TPU v7x, 32 devices: a whole 2x2x4 slice. The times are simulated.
32 devices in a mesh: gx: 2 (over core), gy: 4 (over y, x), lev: 4 (over z).
Axes of the slice: x: 2, y: 2, z: 4, core: 2. Of those that a mesh axis runs over, the one named last changes fastest.
Arguments:
- u_wind: float32 [256, 32, 512], P('lev', 'gx', 'gy'), may hold values from -6 to 6
- v_wind: float32 [256, 32, 512], P('lev', 'gx', 'gy'), may hold values from -6 to 6
- w_wind: float32 [256, 32, 512], P('lev', 'gx', 'gy'), may hold values from -4 to 4
- pressure: float32 [256, 32, 512], P('lev', 'gx', 'gy'), may hold values from -6 to 6
- buoyancy: float32 [256, 32, 512], P('lev', 'gx', 'gy'), may hold values from 0.5 to 2
- stiffness: float32 [256, 32, 512], P('lev', 'gx', 'gy'), may hold values from 0.5 to 2
Outputs:
- u_final: float32 [256, 32, 512], P('lev', 'gx', 'gy')
- v_final: float32 [256, 32, 512], P('lev', 'gx', 'gy')
- w_final: float32 [256, 32, 512], P('lev', 'gx', 'gy')
- p_final: float32 [256, 32, 512], P('lev', 'gx', 'gy')
All inputs are finite; a program needn't handle non-finite values.
Results may differ from a plain program's by a relative error of at most 0.002.
Values sent between devices are 32-bit elements; how exact they have to be, the bound alone decides.
A program may use at most 128 MiB of HBM per device.

v0:
```python
import functools

import jax
import jax.numpy as jnp
from jax import lax
from jax.experimental import pallas as pl
from jax.experimental.pallas import tpu as pltpu
from jax.sharding import PartitionSpec as P

SUBSTEPS = 3
CH = 0.3
GAIN = 4096.0
MESH = pl.DeviceIdType.MESH
GROUP = 16
F32 = jnp.float32


def kernel(
    K, nx, ny, nz,
    u_in, v_in, w_in, p_in, b_in, s_in,
    uo, vo, w, p,
    us, vs, s, bi, bj, E, D, H, X, Y, ps, h,
    i_low, i_high, i_from_up, i_from_down,
    j_own, j_to_right, j_to_left, j_from_left, j_from_right,
    hu, hbi, hv, hbj, C, vbr,
    cmine, cgath, fmine, fgath, red, mine,
    in_sem, hs_sem, hr_sem, cs_sem, cr_sem, ls_sem, lr_sem,
):
    gx, gy, me = lax.axis_index("gx"), lax.axis_index("gy"), lax.axis_index("lev")
    up, down = lax.rem(gx + 1, nx), lax.rem(gx + nx - 1, nx)
    right, left = lax.rem(gy + 1, ny), lax.rem(gy + ny - 1, ny)
    groups = K // GROUP
    K2, KJ, KH = 2 * K, 8 * (K // GROUP), 4 * (K // GROUP)

    loads = []
    for n, (src, dst) in enumerate(
        ((p_in, p), (b_in, bi), (u_in, us), (v_in, vs), (s_in, s), (w_in, w))
    ):
        c = pltpu.make_async_copy(src, dst, in_sem.at[n])
        c.start()
        loads.append(c)

    barrier = pltpu.get_barrier_semaphore()
    for dev in (up, down):
        pl.semaphore_signal(barrier, inc=1, device_id={"gx": dev}, device_id_type=MESH)
    for dev in (left, right):
        pl.semaphore_signal(barrier, inc=1, device_id={"gy": dev}, device_id_type=MESH)
    for o in range(1, nz):
        pl.semaphore_signal(
            barrier, inc=1, device_id={"lev": lax.rem(me + o, nz)}, device_id_type=MESH
        )

    lane = lax.broadcasted_iota(jnp.int32, (8, 128), 1)
    sub = lax.broadcasted_iota(jnp.int32, (8, 128), 0)
    quad = lane % 4

    def roll(x, shift, axis):
        shift = shift % x.shape[axis]
        return x if shift == 0 else pltpu.roll(x, shift, axis)

    def at(ref, row, aligned=True):
        return ref[pl.ds(pl.multiple_of(row, 8) if aligned else row, 8), :]

    def put(ref, row, value):
        ref[pl.ds(pl.multiple_of(row, 8), 8), :] = value

    def each(body, carry=None, downward=False):
        def step(n, c):
            g = groups - 1 - n if downward else n
            return body(g, c)
        return lax.fori_loop(0, groups, step, carry)

    def pair(ref, g, j):
        return at(ref, g * 256 + 16 * j), at(ref, g * 256 + 16 * j + 8)

    def put_pair(ref, g, j, value):
        put(ref, g * 256 + 16 * j, value[0])
        put(ref, g * 256 + 16 * j + 8, value[1])

    def pack_edges(g, j, x, acc, ilo, ihi, f):
        row = 8 + f * K2 + g * 32 + 2 * j
        ilo[pl.ds(row, 2), :] = x[0][0:2]
        ihi[pl.ds(row, 2), :] = x[1][6:8]
        return pack_columns(j, x, acc)

    def pack_columns(j, x, acc):
        for half in range(2):
            q = 2 * j + half
            acc = jnp.where(lane // 4 == q, roll(x[half], 4 * q + 2, 1), acc)
        return acc

    zero = jnp.zeros((8, 128), F32)

    for c in loads[:4]:
        c.wait()

    def first_pack(g, carry):
        accp = accb = accv = zero
        for j in range(GROUP):
            accp = pack_edges(g, j, pair(p, g, j), accp, i_low.at[0], i_high.at[0], 0)
            xb = pair(bi, g, j)
            accb = pack_edges(g, j, xb, accb, i_low.at[0], i_high.at[0], 1)
            xu = pair(us, g, j)
            row = 8 + 2 * K2 + g * 32 + 2 * j
            i_low[0, pl.ds(row, 2), :] = xu[0][0:2]
            i_high[0, pl.ds(row, 2), :] = xu[1][6:8]
            accv = pack_columns(j, pair(vs, g, j), accv)
        j_own[0, pl.ds(pl.multiple_of(g * 8, 8), 8), :] = accp
        j_own[0, pl.ds(pl.multiple_of(KJ + g * 8, 8), 8), :] = accb
        j_own[0, pl.ds(pl.multiple_of(2 * KJ + g * 8, 8), 8), :] = accv
        return carry

    each(first_pack, 0)

    def dense(t, f):
        for n in range(groups // 2):
            a, b = (j_own[t, 16 * n + 8 * m:16 * n + 8 * m + 8, :] for m in range(2))
            j_to_right[t, 8 * n:8 * n + 8, :] = jnp.where(quad < 2, a, roll(b, 2, 1))
            j_to_left[t, 8 * n:8 * n + 8, :] = jnp.where(quad < 2, roll(a, -2, 1), b)
            if f:
                rights, lefts = [], []
                for m in range(2):
                    k = 16 * n + 8 * m
                    ab = j_own[t, KJ + k:KJ + k + 8, :]
                    av = j_own[t, 2 * KJ + k:2 * KJ + k + 8, :]
                    rights.append(jnp.where(quad == 0, roll(av, -1, 1), ab))
                    lefts.append(jnp.where(quad == 0, roll(av, -2, 1), roll(ab, -1, 1)))
                k = KH + 8 * n
                for ref, (a, b) in ((j_to_right, rights), (j_to_left, lefts)):
                    ref[t, k:k + 8, :] = jnp.where(quad < 2, a, roll(b, 2, 1))

    dense(0, True)
    pl.semaphore_wait(barrier, 4 + nz - 1)

    def halo_copies(t):
        ri = pl.ds(8, (3 if t == 0 else 1) * K2)
        rj = pl.ds(0, (2 if t == 0 else 1) * KH)
        return [
            pltpu.make_async_remote_copy(
                src_ref=src.at[t, rows], dst_ref=dst.at[t, rows],
                send_sem=hs_sem.at[t, n], recv_sem=hr_sem.at[t, n],
                device_id={axis: dev}, device_id_type=MESH,
            )
            for n, (src, dst, rows, axis, dev) in enumerate((
                (j_to_right, j_from_left, rj, "gy", right),
                (j_to_left, j_from_right, rj, "gy", left),
                (i_low, i_from_up, ri, "gx", down),
                (i_high, i_from_down, ri, "gx", up),
            ))
        ]

    halos = halo_copies(0)
    for c in halos:
        c.start()

    def lev_copies(src, gath, send, recv):
        return [
            pltpu.make_async_remote_copy(
                src_ref=src(lax.div(me + o, nz)), dst_ref=gath.at[me],
                send_sem=send.at[o - 1], recv_sem=recv.at[o - 1],
                device_id={"lev": lax.rem(me + o, nz)}, device_id_type=MESH,
            )
            for o in range(1, nz)
        ]

    loads[4].wait()

    def factor(g, carry):
        B, Z = carry
        for j in reversed(range(GROUP)):
            bb, ss = pair(bi, g, j), pair(s, g, j)
            newB, newZ = [], []
            for m in range(2):
                row = g * 256 + 16 * j + 8 * m
                gb = GAIN * bb[m]
                one = 1.0 + gb * B[m]
                d = 1.0 / (one + gb * ss[m])
                hh = gb * d
                e = hh * ss[m]
                put(D, row, d)
                put(H, row, hh)
                put(E, row, e)
                put(Y, row, hh * Z[m])
                newB.append(ss[m] * (one * d))
                newZ.append(e * Z[m])
            B, Z = tuple(newB), tuple(newZ)
        return B, Z

    one = jnp.ones((8, 128), F32)
    B, Z = each(factor, ((zero, zero), (one, one)), downward=True)

    def responses(g, carry):
        x, y = carry
        for j in range(GROUP):
            ee, hz = pair(E, g, j), pair(Y, g, j)
            x = tuple(ee[m] * x[m] for m in range(2))
            y = tuple(ee[m] * y[m] - hz[m] for m in range(2))
            put_pair(X, g, j, x)
            put_pair(Y, g, j, y)
        return x, y

    x, y = each(responses, ((one, one), (zero, zero)))
    for n, val in enumerate((x, y, Z, B)):
        for m in range(2):
            cmine[16 * n + 8 * m:16 * n + 8 * m + 8, :] = val[m]
            cgath[me, 16 * n + 8 * m:16 * n + 8 * m + 8, :] = val[m]
    consts = lev_copies(lambda below: cmine, cgath, cs_sem, cr_sem)
    for c in consts:
        c.start()

    def crow(d, n):
        return cgath[d, 16 * n:16 * n + 16, :]

    for c in halos:
        c.wait()

    def halo_rows(ref, t, f, g, j, sublane):
        return ref[t, pl.ds(8 + f * K2 + g * 32 + 2 * j - sublane, 8), :]

    for n in range(groups // 2):
        fr = j_from_right[0, KH + 8 * n:KH + 8 * n + 8, :]
        fl = j_from_left[0, KH + 8 * n:KH + 8 * n + 8, :]
        for m in range(2):
            k = 16 * n + 8 * m
            vbr[k:k + 8, :] = roll(fr, -2 * m, 1)
            flg = roll(fl, -2 * m, 1)
            ab = j_own[0, KJ + k:KJ + k + 8, :]
            av = j_own[0, 2 * KJ + k:2 * KJ + k + 8, :]
            hv[k:k + 8, :] = jnp.where(quad == 2, roll(flg, 2, 1), roll(av, 1, 1))
            hbj[k:k + 8, :] = CH * roll(jnp.where(quad == 1, flg, ab), 1, 1)

    def stagger(g, carry):
        packed = at(vbr, g * 8)
        for j in range(GROUP):
            xb, xu, xv = pair(bi, g, j), pair(us, g, j), pair(vs, g, j)
            for (val, dst, scale, f) in ((xu, us, 1.0, 2), (xb, bi, CH, 1)):
                r0, r1 = roll(val[0], 7, 0), roll(val[1], 7, 0)
                edge = halo_rows(i_from_up, 0, f, g, j, 7)
                put_pair(dst, g, j, (
                    scale * jnp.where(sub < 7, r0, r1), scale * jnp.where(sub < 7, r1, edge)
                ))
            for (val, dst, scale, first) in ((xv, vs, 1.0, 127), (xb, bj, CH, 126)):
                out = []
                for m in range(2):
                    q = 2 * j + m
                    out.append(scale * jnp.where(
                        lane == 127, roll(packed, first - 4 * q, 1), roll(val[m], 127, 1)
                    ))
                put_pair(dst, g, j, out)
        for r in range(4):
            row = g * 32 + 8 * r
            for (dst, f, scale) in ((hu, 2, 1.0), (hbi, 1, CH)):
                base = 8 + f * K2 + row
                below = i_from_down[0, pl.ds(base + 1, 8), :]
                own = i_low[0, pl.ds(base - 1, 8), :]
                put(dst, 8 + row, scale * jnp.where(sub % 2 == 0, below, own))
        return carry

    each(stagger, 0)

    loads[5].wait()

    for t in range(SUBSTEPS):
        final = t == SUBSTEPS - 1
        if t > 0:
            for c in halos:
                c.wait()

        for n in range(groups // 2):
            fr = j_from_right[t, 8 * n:8 * n + 8, :]
            fl = j_from_left[t, 8 * n:8 * n + 8, :]
            for m in range(2):
                k = 16 * n + 8 * m
                before = roll(fl, 2, 1) if m == 0 else fl
                own = j_own[t, k:k + 8, :]
                hv_new = hv[k:k + 8, :] - hbj[k:k + 8, :] * (own - before)
                hv[k:k + 8, :] = hv_new
                C[k:k + 8, :] = jnp.where(quad < 2, roll(fr, -2 * m, 1), hv_new)

        def explicit(g, A):
            for r in range(4):
                row = g * 32 + 8 * r
                low = i_low[t, pl.ds(pl.multiple_of(8 + row, 8), 8), :]
                below = i_from_down[t, pl.ds(pl.multiple_of(8 + row, 8), 8), :]
                put(hu, 8 + row, at(hu, 8 + row) - at(hbi, 8 + row) * (low - below))
            c = at(C, g * 8)
            for j in reversed(range(GROUP)):
                pp, uu, vv, ww = pair(p, g, j), pair(us, g, j), pair(vs, g, j), pair(w, g, j)
                bbi, bbj, ss = pair(bi, g, j), pair(bj, g, j), pair(s, g, j)
                ee, dd, hh = pair(E, g, j), pair(D, g, j), pair(H, g, j)
                r0, r1 = roll(pp[0], 6, 0), roll(pp[1], 6, 0)
                edge = halo_rows(i_from_up, t, 0, g, j, 6)
                pi = (jnp.where(sub < 6, r0, r1), jnp.where(sub < 6, r1, edge))
                un = tuple(uu[m] - bbi[m] * (pi[m] - pp[m]) for m in range(2))
                put_pair(us, g, j, un)
                r0, r1 = roll(un[0], 2, 0), roll(un[1], 2, 0)
                edge = at(hu, 8 + g * 32 + 2 * j, False)
                um = (jnp.where(sub < 2, edge, r0), jnp.where(sub < 2, r0, r1))
                newA, hs, pss, vn = [], [], [], []
                for m in range(2):
                    edge = roll(c, 126 - 4 * (2 * j + m), 1)
                    pj = jnp.where(lane >= 126, edge, roll(pp[m], 126, 1))
                    v_new = vv[m] - bbj[m] * (pj - pp[m])
                    vm = jnp.where(lane < 2, edge, roll(v_new, 2, 1))
                    star = pp[m] - (CH * ss[m]) * ((un[m] - um[m]) + (v_new - vm))
                    dw = dd[m] * ww[m]
                    hs.append(dw + hh[m] * (star - A[m]))
                    newA.append(ee[m] * A[m] + ((star - ee[m] * star) - ss[m] * dw))
                    pss.append(star)
                    vn.append(v_new)
                put_pair(vs, g, j, vn)
                put_pair(ps, g, j, pss)
                put_pair(h, g, j, hs)
                A = tuple(newA)
            return A

        A = each(explicit, (zero, zero), downward=True)

        def forward(g, x):
            for j in range(GROUP):
                ee, hh = pair(E, g, j), pair(h, g, j)
                x = tuple(ee[m] * x[m] + hh[m] for m in range(2))
                put_pair(w, g, j, x)
            return x

        x = each(forward, (zero, zero))
        if t == 0:
            for c in consts:
                c.wait()
            nothing = jnp.zeros((16, 128), F32)
            picks = {name: nothing for name in ("psi", "r2", "beta", "r", "wa", "aw", "lam")}

            def pick(name, d, val):
                picks[name] = jnp.where(me == d, val, picks[name])

            beta = nothing
            betas = [None] * nz
            for d in range(nz - 1, -1, -1):
                R = 1.0 / (1.0 - crow(d, 1) * beta)
                zbr = crow(d, 2) * beta * R
                lam = crow(d, 2) + zbr * crow(d, 1)
                red[d, 0:16, :] = lam
                for name, val in (("beta", beta), ("r", R), ("aw", zbr), ("lam", lam)):
                    pick(name, d, val)
                beta = crow(d, 3) + zbr * crow(d, 0)
                betas[d] = beta
            psi = nothing
            for d in range(nz):
                xr = crow(d, 0) / (1.0 - psi * crow(d, 3))
                xrp = xr * psi
                red[d, 16:32, :] = xr
                pick("psi", d, psi)
                pick("r2", d, 1.0 / (1.0 - psi * betas[d]))
                pick("wa", d, xrp)
                psi = crow(d, 1) + xrp * crow(d, 2)
            for n, name in enumerate(picks):
                mine[16 * n:16 * n + 16, :] = picks[name]

        psi, r2, beta, r, wa, aw, lam = (mine[16 * n:16 * n + 16, :] for n in range(7))
        A0, W0 = (jnp.concatenate(q, 0) for q in (A, x))
        up_row, down_row = W0 + wa * A0, A0 + aw * W0
        fmine[t, 0], fmine[t, 1] = up_row, down_row
        sends = lev_copies(lambda below: fmine.at[t, below], fgath.at[t], ls_sem.at[t], lr_sem.at[t])
        for c in sends:
            c.start()

        if final:
            def emit(g, carry):
                hvg = at(hv, pl.multiple_of(g * 8, 8))
                for j in range(GROUP):
                    uu, vv = pair(us, g, j), pair(vs, g, j)
                    r0, r1 = roll(uu[0], 1, 0), roll(uu[1], 1, 0)
                    edge = at(hu, 8 + g * 32 + 2 * j + 1, False)
                    put_pair(uo, g, j, (jnp.where(sub < 1, edge, r0), jnp.where(sub < 1, r0, r1)))
                    put_pair(vo, g, j, [
                        jnp.where(
                            lane == 0, roll(hvg, 125 - 4 * (2 * j + m), 1), roll(vv[m], 1, 1)
                        )
                        for m in range(2)
                    ])
                return carry

            each(emit, 0)
        for c in sends:
            c.wait()

        omega = alpha = jnp.zeros((16, 128), F32)
        for d in range(nz - 1):
            omega = jnp.where(me > d, fgath[t, d] + red[d, 16:32, :] * omega, omega)
        for d in range(nz - 1, 0, -1):
            alpha = jnp.where(me < d, fgath[t, d] + red[d, 0:16, :] * alpha, alpha)
        wb = r2 * (omega + psi * (down_row + lam * alpha))
        pa = alpha + beta * (r * (W0 + crow(me, 1) * alpha + crow(me, 0) * wb))
        wb2, pa2 = (wb[0:8], wb[8:16]), (pa[0:8], pa[8:16])

        def implicit(g, wprev):
            acc = zero
            for j in range(GROUP):
                w0, xx, yy = pair(w, g, j), pair(X, g, j), pair(Y, g, j)
                ss, star = pair(s, g, j), pair(ps, g, j)
                wn = tuple(w0[m] + xx[m] * wb2[m] + yy[m] * pa2[m] for m in range(2))
                pn = tuple(star[m] - ss[m] * (wn[m] - wprev[m]) for m in range(2))
                put_pair(w, g, j, wn)
                put_pair(p, g, j, pn)
                if not final:
                    acc = pack_edges(g, j, pn, acc, i_low.at[t + 1], i_high.at[t + 1], 0)
                wprev = wn
            if not final:
                j_own[t + 1, pl.ds(pl.multiple_of(g * 8, 8), 8), :] = acc
            return wprev

        each(implicit, wb2)
        if not final:
            dense(t + 1, False)
            halos = halo_copies(t + 1)
            for c in halos:
                c.start()


def store(u, v, w, p, u_out, v_out, w_out, p_out, sem):
    copies = [
        pltpu.make_async_copy(src, dst, sem.at[n])
        for n, (src, dst) in enumerate(((u, u_out), (v, v_out), (w, w_out), (p, p_out)))
    ]
    for c in copies:
        c.start()
    for c in copies:
        c.wait()


def solution(mesh):
    nx, ny, nz = (mesh.shape[a] for a in ("gx", "gy", "lev"))

    def shards(*fields):
        K, I, J = fields[0].shape
        assert I == 16 and J == 128 and K % (2 * GROUP) == 0
        R, KJ, T = K * I, 8 * (K // GROUP), SUBSTEPS
        full = pltpu.VMEM((R, J), F32)
        ihalo = pltpu.VMEM((T, 6 * K + 16, J), F32)
        jhalo = pltpu.VMEM((T, 3 * KJ, J), F32)
        jdense = pltpu.VMEM((T, KJ, J), F32)
        outs = pl.pallas_call(
            functools.partial(kernel, K, nx, ny, nz),
            out_shape=[full] * 4,
            in_specs=[pl.BlockSpec(memory_space=pl.ANY)] * 6,
            out_specs=[pl.BlockSpec(memory_space=pltpu.VMEM)] * 4,
            scratch_shapes=[full] * 12 + [ihalo] * 4 + [jhalo] + [jdense] * 4 + [
                pltpu.VMEM((2 * K + 16, J), F32),
                pltpu.VMEM((2 * K + 16, J), F32),
                pltpu.VMEM((KJ, J), F32),
                pltpu.VMEM((KJ, J), F32),
                pltpu.VMEM((KJ, J), F32),
                pltpu.VMEM((KJ, J), F32),
                pltpu.VMEM((64, J), F32),
                pltpu.VMEM((nz, 64, J), F32),
                pltpu.VMEM((T, 2, 16, J), F32),
                pltpu.VMEM((T, nz, 16, J), F32),
                pltpu.VMEM((nz, 32, J), F32),
                pltpu.VMEM((112, J), F32),
                pltpu.SemaphoreType.DMA((6,)),
                pltpu.SemaphoreType.DMA((T, 4)),
                pltpu.SemaphoreType.DMA((T, 4)),
                pltpu.SemaphoreType.DMA((max(nz - 1, 1),)),
                pltpu.SemaphoreType.DMA((max(nz - 1, 1),)),
                pltpu.SemaphoreType.DMA((T, max(nz - 1, 1))),
                pltpu.SemaphoreType.DMA((T, max(nz - 1, 1))),
            ],
            compiler_params=pltpu.CompilerParams(collective_id=0, has_side_effects=True),
        )(*(f.reshape(R, J) for f in fields))
        outs = pl.pallas_call(
            store,
            out_shape=[jax.ShapeDtypeStruct((R, J), F32)] * 4,
            in_specs=[pl.BlockSpec(memory_space=pltpu.VMEM)] * 4,
            out_specs=[pl.BlockSpec(memory_space=pl.ANY)] * 4,
            scratch_shapes=[pltpu.SemaphoreType.DMA((4,))],
        )(*(pltpu.with_memory_space_constraint(o, pltpu.VMEM) for o in outs))
        return tuple(o.reshape(K, I, J) for o in outs)

    spec = P("lev", "gx", "gy")
    return jax.shard_map(
        shards, mesh=mesh, in_specs=(spec,) * 6, out_specs=(spec,) * 4, check_vma=False
    )
```

profile of v0, /device:TPU:0, one launch (start us, length us, event | category | flops | bytes accessed | tf_op | source)
XLA Modules:
  0.0 34.9 jit_solution(2134483242225016414)
XLA Ops:
  0.6 32.9 %shard_map.93 = (f32[1024,128]{1,0:T(8,128)S(1)}, f32[1024,128]{1,0:T(8,128)S(1)}, f32[1024,128]{1,0:T(8,128)S(1)}, f32[1024,128]{1,0:T(8,128)S(1)}) custom-call(f32[1024,128]{1,0:T(8,128)} %bitcast.10, f32[1024,128]{1,0:T(8,128)} %bitcast.11, f32[1024,128]{1,0:T(8,128)} %bitcast.12, f32[1024,128]{1,0:T(8,128)} %bitcast.13, f32[1024,128]{1,0:T(8,128)} %bitcast.14, ...), custom_call_target="tpu_custom_call" | custom-call | tf_op jit(solution)/shard_map/pallas_call | solution.py:442
  33.5 1.3 %shard_map.94 = (f32[1024,128]{1,0:T(8,128)}, f32[1024,128]{1,0:T(8,128)}, f32[1024,128]{1,0:T(8,128)}, f32[1024,128]{1,0:T(8,128)}) custom-call(f32[1024,128]{1,0:T(8,128)S(1)} %get-tuple-element.12.u, f32[1024,128]{1,0:T(8,128)S(1)} %get-tuple-element.13.v, f32[1024,128]{1,0:T(8,128)S(1)} %get-tuple-element.14.w, f32[1024,128]{1,0:T(8,128)S(1)} %get-tuple-element.15.p), custom_call_target="tpu_custom_call" | custom-call | tf_op jit(solution)/shard_map/pallas_call | solution.py:470
where the time goes:
time: 35 us; the launch traced here: 34.9 us
  Pallas kernels  34.2 us (98%)
  between operations  0.64 us (2%)
    pallas_call x1, Pallas kernels, shards(): pl.pallas_call(functools.partial(kernel, K, nx, ny, nz), out_shape=[full]...  32.9 us
    pallas_call x1, Pallas kernels, shards(): pl.pallas_call(store, out_shape=[jax.ShapeDtypeStruct((R, J), F32)] * 4,...  1.35 us

commit v1 on v0

v1 whole, which is shorter than its diff:
```python
import functools
from types import SimpleNamespace

import jax
import jax.numpy as jnp
from jax import lax
from jax.experimental import pallas as pl
from jax.experimental.pallas import tpu as pltpu
from jax.sharding import PartitionSpec as P

SUBSTEPS = 3
CH = 0.3
GAIN = 4096.0
MESH = pl.DeviceIdType.MESH
GROUP = 16
F32 = jnp.float32


def scratch(K, J, nz):
    R, T, KJ, K2, KH = 16 * K, SUBSTEPS, 8 * (K // GROUP), 2 * K, 4 * (K // GROUP)
    V = lambda *s: pltpu.VMEM((*s, J), F32)
    D = lambda *s: pltpu.SemaphoreType.DMA(s)
    m = max(nz - 1, 1)
    s = {n: V(R) for n in ("us", "vs", "s", "bi", "bj", "E", "D", "H", "X", "Y", "ps", "h")}
    s |= {n: V(3 * K2 + 16) for n in ("i0_low", "i0_high", "i0_up", "i0_down")}
    s |= {n: V(2 * KH) for n in ("j0_right", "j0_left", "j0_fl", "j0_fr")}
    s |= {n: V(3 * K2) for n in ("is_low", "is_high", "is_up", "is_down")}
    s |= {n: V(3 * KH) for n in ("js_right", "js_left", "js_fl", "js_fr")}
    s |= {n: V(T, 2 * K2) for n in ("iw_low", "iw_high", "iw_up", "iw_down")}
    s |= {n: V(T, 2 * KH) for n in ("jw_right", "jw_left", "jw_fl", "jw_fr")}
    s |= {n: V(T, nz, 8) for n in ("ic_low", "ic_high", "ic_up", "ic_down", "jc", "jc_fl", "jc_fr")}
    s |= {n: V(T, K2 + 16) for n in ("p_up", "p_down", "p_low")}
    s |= {n: V(3 * KJ) for n in ("own0",)}
    s |= {n: V(KJ) for n in ("hv", "hbj", "C", "vbr")}
    s |= {n: V(3 * KJ) for n in ("Hc", "Oc")}
    s |= {n: V(T, 2 * KJ) for n in ("Hw", "Ow")}
    s |= {n: V(T, KJ) for n in ("Hp", "Op")}
    s |= {n: V(K2 + 16) for n in ("hu", "hbi")}
    s |= {"cmine": V(64), "cgath": V(nz, 64), "fmine": V(T, 2, 16), "fgath": V(T, nz, 16)}
    s |= {"ctab": V(nz * nz, 32), "mine": V(80)}
    s |= {"in_sem": D(6)}
    for n in ("h0", "hs"):
        s |= {n + "_s": D(4), n + "_r": D(4)}
    s |= {"hw_s": D(T, 4), "hw_r": D(T, 4), "hc_s": D(T, 4, nz), "hc_r": D(T, 4, nz)}
    s |= {"cs_s": D(m), "cs_r": D(m), "ls_s": D(T, m), "ls_r": D(T, m)}
    return s


def kernel(names, K, nx, ny, nz, u_in, v_in, w_in, p_in, b_in, s_in, uo, vo, w, p, *refs):
    q = SimpleNamespace(**dict(zip(names, refs)))
    gx, gy, me = lax.axis_index("gx"), lax.axis_index("gy"), lax.axis_index("lev")
    up, down = lax.rem(gx + 1, nx), lax.rem(gx + nx - 1, nx)
    right, left = lax.rem(gy + 1, ny), lax.rem(gy + ny - 1, ny)
    groups = K // GROUP
    K2, KJ, KH = 2 * K, 8 * (K // GROUP), 4 * (K // GROUP)
    sides = ({"gy": right}, {"gy": left}, {"gx": down}, {"gx": up})

    loads = []
    for n, (src, dst) in enumerate(
        ((p_in, p), (b_in, q.bi), (u_in, q.us), (v_in, q.vs), (s_in, q.s), (w_in, w))
    ):
        c = pltpu.make_async_copy(src, dst, q.in_sem.at[n])
        c.start()
        loads.append(c)

    barrier = pltpu.get_barrier_semaphore()
    for dev in sides:
        pl.semaphore_signal(barrier, inc=1, device_id=dev, device_id_type=MESH)
    for o in range(1, nz):
        pl.semaphore_signal(
            barrier, inc=1, device_id={"lev": lax.rem(me + o, nz)}, device_id_type=MESH
        )

    lane = lax.broadcasted_iota(jnp.int32, (8, 128), 1)
    sub = lax.broadcasted_iota(jnp.int32, (8, 128), 0)
    quad = lane % 4
    zero = jnp.zeros((8, 128), F32)
    one = jnp.ones((8, 128), F32)

    def roll(x, shift, axis):
        shift = shift % x.shape[axis]
        return x if shift == 0 else pltpu.roll(x, shift, axis)

    def at(ref, row, aligned=True):
        return ref[pl.ds(pl.multiple_of(row, 8) if aligned else row, 8), :]

    def put(ref, row, value):
        ref[pl.ds(pl.multiple_of(row, 8), 8), :] = value

    def each(body, carry=None, downward=False):
        def step(n, c):
            g = groups - 1 - n if downward else n
            return body(g, c)
        return lax.fori_loop(0, groups, step, carry)

    def pair(ref, g, j):
        return at(ref, g * 256 + 16 * j), at(ref, g * 256 + 16 * j + 8)

    def put_pair(ref, g, j, value):
        put(ref, g * 256 + 16 * j, value[0])
        put(ref, g * 256 + 16 * j + 8, value[1])

    def edge_rows(g, j, x, low, high, base):
        row = base + g * 32 + 2 * j
        low[pl.ds(row, 2), :] = x[0][0:2]
        if high is not None:
            high[pl.ds(row, 2), :] = x[1][6:8]

    def pack_columns(j, x, acc):
        for half in range(2):
            n = 2 * j + half
            acc = jnp.where(lane // 4 == n, roll(x[half], 4 * n + 2, 1), acc)
        return acc

    def remote(src, dst, ss, rs, dev):
        return pltpu.make_async_remote_copy(
            src_ref=src, dst_ref=dst, send_sem=ss, recv_sem=rs, device_id=dev, device_id_type=MESH
        )

    def dense(own, base, to_right, to_left, row):
        for n in range(groups // 2):
            a, b = (own[base + 16 * n + 8 * m:base + 16 * n + 8 * m + 8, :] for m in range(2))
            to_right[row + 8 * n:row + 8 * n + 8, :] = jnp.where(quad < 2, a, roll(b, 2, 1))
            to_left[row + 8 * n:row + 8 * n + 8, :] = jnp.where(quad < 2, roll(a, -2, 1), b)

    def open_up(fl, fr, row, dst, base):
        for n in range(groups // 2):
            a, b = fl[row + 8 * n:row + 8 * n + 8, :], fr[row + 8 * n:row + 8 * n + 8, :]
            for m in range(2):
                k = base + 16 * n + 8 * m
                dst[k:k + 8, :] = jnp.where(
                    quad < 2, roll(b, -2 * m, 1), roll(a, 2, 1) if m == 0 else a
                )

    for c in loads[:4]:
        c.wait()

    def first_pack(g, carry):
        accp = accb = accv = zero
        for j in range(GROUP):
            for n, ref in enumerate((p, q.bi, q.us)):
                x = pair(ref, g, j)
                edge_rows(g, j, x, q.i0_low, q.i0_high, 8 + n * K2)
                if n == 0:
                    accp = pack_columns(j, x, accp)
                if n == 1:
                    accb = pack_columns(j, x, accb)
            accv = pack_columns(j, pair(q.vs, g, j), accv)
        put(q.own0, g * 8, accp)
        put(q.own0, KJ + g * 8, accb)
        put(q.own0, 2 * KJ + g * 8, accv)
        return carry

    each(first_pack, 0)

    dense(q.own0, 0, q.j0_right, q.j0_left, 0)
    for n in range(groups // 2):
        rights, lefts = [], []
        for m in range(2):
            k = 16 * n + 8 * m
            ab = q.own0[KJ + k:KJ + k + 8, :]
            av = q.own0[2 * KJ + k:2 * KJ + k + 8, :]
            rights.append(jnp.where(quad == 0, roll(av, -1, 1), ab))
            lefts.append(jnp.where(quad == 0, roll(av, -2, 1), roll(ab, -1, 1)))
        k = KH + 8 * n
        for ref, (a, b) in ((q.j0_right, rights), (q.j0_left, lefts)):
            ref[k:k + 8, :] = jnp.where(quad < 2, a, roll(b, 2, 1))

    pl.semaphore_wait(barrier, 4 + nz - 1)

    def exchange(name, ss, rs, at_=lambda r: r):
        return [
            remote(at_(getattr(q, name + a)), at_(getattr(q, name + b)), ss(n), rs(n), dev)
            for n, (a, b, dev) in enumerate(zip(
                ("_right", "_left", "_low", "_high"), ("_fl", "_fr", "_up", "_down"), sides
            ))
        ]

    def four(i, j, ss, rs, at_=lambda r: r):
        pairs = (
            (j + "_right", j + "_fl"), (j + "_left", j + "_fr"),
            (i + "_low", i + "_up"), (i + "_high", i + "_down"),
        )
        return [
            remote(at_(getattr(q, a)), at_(getattr(q, b)), ss(n), rs(n), dev)
            for n, ((a, b), dev) in enumerate(zip(pairs, sides))
        ]

    rows0 = pl.ds(8, 3 * K2)
    halos = [
        remote(
            a if n < 2 else a.at[rows0], b if n < 2 else b.at[rows0],
            q.h0_s.at[n], q.h0_r.at[n], dev,
        )
        for n, (a, b, dev) in enumerate(zip(
            (q.j0_right, q.j0_left, q.i0_low, q.i0_high),
            (q.j0_fl, q.j0_fr, q.i0_up, q.i0_down), sides,
        ))
    ]
    for c in halos:
        c.start()

    loads[4].wait()

    def factor(g, carry):
        B, Z = carry
        for j in reversed(range(GROUP)):
            bb, ss = pair(q.bi, g, j), pair(q.s, g, j)
            newB, newZ = [], []
            for m in range(2):
                row = g * 256 + 16 * j + 8 * m
                gb = GAIN * bb[m]
                o = 1.0 + gb * B[m]
                d = 1.0 / (o + gb * ss[m])
                hh = gb * d
                e = hh * ss[m]
                put(q.D, row, d)
                put(q.H, row, hh)
                put(q.E, row, e)
                put(q.Y, row, hh * Z[m])
                newB.append(ss[m] * (o * d))
                newZ.append(e * Z[m])
            B, Z = tuple(newB), tuple(newZ)
        return B, Z

    B, Z = each(factor, ((zero, zero), (one, one)), downward=True)

    def responses(g, carry):
        x, y = carry
        accs = [zero] * 3
        for j in range(GROUP):
            ee, hz = pair(q.E, g, j), pair(q.Y, g, j)
            x = tuple(ee[m] * x[m] for m in range(2))
            y = tuple(ee[m] * y[m] - hz[m] for m in range(2))
            put_pair(q.X, g, j, x)
            put_pair(q.Y, g, j, y)
            for n, val in enumerate((pair(q.s, g, j), x, y)):
                edge_rows(g, j, val, q.is_low, q.is_high, n * K2)
                accs[n] = pack_columns(j, val, accs[n])
        for n in range(3):
            put(q.Oc, n * KJ + g * 8, accs[n])
        return x, y

    x, y = each(responses, ((one, one), (zero, zero)))
    for n, val in enumerate((x, y, Z, B)):
        for m in range(2):
            q.cmine[16 * n + 8 * m:16 * n + 8 * m + 8, :] = val[m]
            q.cgath[me, 16 * n + 8 * m:16 * n + 8 * m + 8, :] = val[m]
    consts = [
        remote(q.cmine, q.cgath.at[me], q.cs_s.at[o - 1], q.cs_r.at[o - 1], {"lev": lax.rem(me + o, nz)})
        for o in range(1, nz)
    ]
    for c in consts:
        c.start()
    for n in range(3):
        dense(q.Oc, n * KJ, q.js_right, q.js_left, n * KH)
    setups = four("is", "js", lambda n: q.hs_s.at[n], lambda n: q.hs_r.at[n])
    for c in setups:
        c.start()

    def crow(d, n):
        return q.cgath[d, 16 * n:16 * n + 16, :]

    for c in halos:
        c.wait()

    for n in range(groups // 2):
        fr = q.j0_fr[KH + 8 * n:KH + 8 * n + 8, :]
        fl = q.j0_fl[KH + 8 * n:KH + 8 * n + 8, :]
        for m in range(2):
            k = 16 * n + 8 * m
            q.vbr[k:k + 8, :] = roll(fr, -2 * m, 1)
            flg = roll(fl, -2 * m, 1)
            ab = q.own0[KJ + k:KJ + k + 8, :]
            av = q.own0[2 * KJ + k:2 * KJ + k + 8, :]
            q.hv[k:k + 8, :] = jnp.where(quad == 2, roll(flg, 2, 1), roll(av, 1, 1))
            q.hbj[k:k + 8, :] = CH * roll(jnp.where(quad == 1, flg, ab), 1, 1)
    open_up(q.j0_fl, q.j0_fr, 0, q.Hp.at[0], 0)

    def stagger(g, carry):
        packed = at(q.vbr, g * 8)
        for j in range(GROUP):
            xb, xu, xv = pair(q.bi, g, j), pair(q.us, g, j), pair(q.vs, g, j)
            for (val, dst, scale, f) in ((xu, q.us, 1.0, 2), (xb, q.bi, CH, 1)):
                r0, r1 = roll(val[0], 7, 0), roll(val[1], 7, 0)
                edge = q.i0_up[pl.ds(8 + f * K2 + g * 32 + 2 * j - 7, 8), :]
                put_pair(dst, g, j, (
                    scale * jnp.where(sub < 7, r0, r1), scale * jnp.where(sub < 7, r1, edge)
                ))
            for (val, dst, scale, first) in ((xv, q.vs, 1.0, 127), (xb, q.bj, CH, 126)):
                out = []
                for m in range(2):
                    n = 2 * j + m
                    out.append(scale * jnp.where(
                        lane == 127, roll(packed, first - 4 * n, 1), roll(val[m], 127, 1)
                    ))
                put_pair(dst, g, j, out)
        for r in range(4):
            row = g * 32 + 8 * r
            for (dst, f, scale) in ((q.hu, 2, 1.0), (q.hbi, 1, CH)):
                base = 8 + f * K2 + row
                below = q.i0_down[pl.ds(base + 1, 8), :]
                own = q.i0_low[pl.ds(base - 1, 8), :]
                put(dst, 8 + row, scale * jnp.where(sub % 2 == 0, below, own))
        return carry

    each(stagger, 0)

    loads[5].wait()

    def interface():
        beta = jnp.zeros((16, 128), F32)
        betas, rs, zbrs, lams = ([None] * nz for _ in range(4))
        for d in range(nz - 1, -1, -1):
            betas[d] = beta
            rs[d] = 1.0 / (1.0 - crow(d, 1) * beta)
            zbrs[d] = crow(d, 2) * beta * rs[d]
            lams[d] = crow(d, 2) + zbrs[d] * crow(d, 1)
            beta = crow(d, 3) + zbrs[d] * crow(d, 0)
            if d == 0:
                last = beta
        tops = [last] + betas[:-1]
        psi = jnp.zeros((16, 128), F32)
        psis, r2s, xrs, xrps = ([None] * nz for _ in range(4))
        for d in range(nz):
            xrs[d] = crow(d, 0) / (1.0 - psi * crow(d, 3))
            xrps[d] = xrs[d] * psi
            psis[d] = psi
            r2s[d] = 1.0 / (1.0 - psi * tops[d])
            psi = crow(d, 1) + xrps[d] * crow(d, 2)

        def pick(vals):
            out = vals[0]
            for d in range(1, nz):
                out = jnp.where(me == d, vals[d], out)
            return out

        br = [betas[d] * rs[d] for d in range(nz)]
        brx = [br[d] * crow(d, 0) for d in range(nz)]
        for n, vals in enumerate((xrps, zbrs, [r2s[d] * psis[d] for d in range(nz)], br, brx)):
            q.mine[16 * n:16 * n + 16, :] = pick(vals)
        for L in range(nz):
            part = r2s[L]
            for d in range(L - 1, -1, -1):
                q.ctab[L * nz + d, 0:16, :] = part
                q.ctab[L * nz + d, 16:32, :] = brx[L] * part
                part = part * xrs[d]
            part, gain = jnp.ones((16, 128), F32), 1.0 + br[L] * crow(L, 1)
            rpl = r2s[L] * psis[L] * lams[L]
            for d in range(L + 1, nz):
                cw = rpl * part
                q.ctab[L * nz + d, 0:16, :] = cw
                q.ctab[L * nz + d, 16:32, :] = part * gain + brx[L] * cw
                part = part * lams[d]

    def halves(x):
        return x[0:8], x[8:16]

    def pack_pair(wx, px):
        (w0, w1), (p0, p1) = halves(wx), halves(px)
        acc = roll(w0, 2, 1)
        for n, val in ((1, w1), (2, p0), (3, p1)):
            acc = jnp.where(lane // 4 == n, roll(val, 4 * n + 2, 1), acc)
        return acc

    def spread(t):
        z = jnp.where(lane < 16, t, 0.0)
        for n in (16, 32, 64):
            z = z + roll(z, n, 1)
        r = roll(z, 8, 1)
        return jnp.where(lane % 16 < 8, z, r), jnp.where(lane % 16 < 8, r, z)

    for t in range(SUBSTEPS):
        final = t == SUBSTEPS - 1
        i_up, i_down, i_low = (
            (q.i0_up, q.i0_down, q.i0_low) if t == 0
            else (q.p_up.at[t - 1], q.p_down.at[t - 1], q.p_low.at[t - 1])
        )
        own_p, own_base = (q.own0, 0) if t == 0 else (q.Op.at[t - 1], 0)
        halo_p = q.Hp.at[t]

        for k in range(0, KJ, 8):
            hp = halo_p[k:k + 8, :]
            hv_new = q.hv[k:k + 8, :] - q.hbj[k:k + 8, :] * (own_p[own_base + k:own_base + k + 8, :] - hp)
            q.hv[k:k + 8, :] = hv_new
            q.C[k:k + 8, :] = jnp.where(quad < 2, hp, hv_new)

        def explicit(g, A):
            for r in range(4):
                row = g * 32 + 8 * r
                put(q.hu, 8 + row, at(q.hu, 8 + row) - at(q.hbi, 8 + row) * (
                    at(i_low, 8 + row) - at(i_down, 8 + row)
                ))
            c = at(q.C, g * 8)
            acc = zero
            for j in reversed(range(GROUP)):
                pp, uu, vv, ww = pair(p, g, j), pair(q.us, g, j), pair(q.vs, g, j), pair(w, g, j)
                bbi, bbj, ss = pair(q.bi, g, j), pair(q.bj, g, j), pair(q.s, g, j)
                ee, dd, hh = pair(q.E, g, j), pair(q.D, g, j), pair(q.H, g, j)
                r0, r1 = roll(pp[0], 6, 0), roll(pp[1], 6, 0)
                edge = at(i_up, 8 + g * 32 + 2 * j - 6, False)
                pi = (jnp.where(sub < 6, r0, r1), jnp.where(sub < 6, r1, edge))
                un = tuple(uu[m] - bbi[m] * (pi[m] - pp[m]) for m in range(2))
                put_pair(q.us, g, j, un)
                r0, r1 = roll(un[0], 2, 0), roll(un[1], 2, 0)
                edge = at(q.hu, 8 + g * 32 + 2 * j, False)
                um = (jnp.where(sub < 2, edge, r0), jnp.where(sub < 2, r0, r1))
                newA, hs, pss, vn = [], [], [], []
                for m in range(2):
                    edge = roll(c, 126 - 4 * (2 * j + m), 1)
                    pj = jnp.where(lane >= 126, edge, roll(pp[m], 126, 1))
                    v_new = vv[m] - bbj[m] * (pj - pp[m])
                    vm = jnp.where(lane < 2, edge, roll(v_new, 2, 1))
                    star = pp[m] - (CH * ss[m]) * ((un[m] - um[m]) + (v_new - vm))
                    dw = dd[m] * ww[m]
                    hs.append(dw + hh[m] * (star - A[m]))
                    newA.append(ee[m] * A[m] + ((star - ee[m] * star) - ss[m] * dw))
                    pss.append(star)
                    vn.append(v_new)
                put_pair(q.vs, g, j, vn)
                put_pair(q.ps, g, j, pss)
                put_pair(q.h, g, j, hs)
                if not final:
                    edge_rows(g, j, pss, q.iw_low.at[t], q.iw_high.at[t], 0)
                    acc = pack_columns(j, pss, acc)
                A = tuple(newA)
            if not final:
                put(q.Ow.at[t], g * 8, acc)
            return A

        A = each(explicit, (zero, zero), downward=True)

        def forward(g, x):
            acc = zero
            for j in range(GROUP):
                ee, hh = pair(q.E, g, j), pair(q.h, g, j)
                x = tuple(ee[m] * x[m] + hh[m] for m in range(2))
                put_pair(w, g, j, x)
                if not final:
                    edge_rows(g, j, x, q.iw_low.at[t], q.iw_high.at[t], K2)
                    acc = pack_columns(j, x, acc)
            if not final:
                put(q.Ow.at[t], KJ + g * 8, acc)
            return x

        x = each(forward, (zero, zero))
        if t == 0:
            for c in consts:
                c.wait()
            interface()

        wa, aw, r2psi, br, brx = (q.mine[16 * n:16 * n + 16, :] for n in range(5))
        A0, W0 = (jnp.concatenate(n, 0) for n in (A, x))
        up_row, down_row = W0 + wa * A0, A0 + aw * W0
        q.fmine[t, 0], q.fmine[t, 1] = up_row, down_row
        sends, peers = [], {}
        for o in range(1, nz):
            peers[o] = remote(
                q.fmine.at[t, lax.div(me + o, nz)], q.fgath.at[t, me],
                q.ls_s.at[t, o - 1], q.ls_r.at[t, o - 1], {"lev": lax.rem(me + o, nz)},
            )
        wb_own = r2psi * down_row
        pa_own = br * W0 + brx * wb_own
        order = sorted(range(nz), key=lambda o: -min(o, nz - o))
        for o in order:
            if not final:
                L = lax.rem(me + o, nz)
                if o:
                    row = q.fmine[t, lax.div(me + o, nz)]
                    wc, pc = (q.ctab[L * nz + me, 16 * n:16 * n + 16, :] * row for n in range(2))
                else:
                    wc, pc = wb_own, pa_own
                q.jc[t, o] = pack_pair(wc, pc)
                q.ic_low[t, o] = jnp.where(sub < 2, wc[0:8], roll(pc[0:8], 2, 0))
                q.ic_high[t, o] = jnp.where(sub < 2, roll(wc[8:16], 2, 0), roll(pc[8:16], 4, 0))
                for n, (a, b) in enumerate((
                    (q.jc, q.jc_fl), (q.jc, q.jc_fr), (q.ic_low, q.ic_up), (q.ic_high, q.ic_down)
                )):
                    c = remote(
                        a.at[t, o], b.at[t, me], q.hc_s.at[t, n, o], q.hc_r.at[t, n, o],
                        {**sides[n], "lev": L},
                    )
                    c.start()
                    sends.append(c)
            if o:
                peers[o].start()
                sends.append(peers[o])
        if not final:
            for n in range(2):
                dense(q.Ow.at[t], n * KJ, q.jw_right.at[t], q.jw_left.at[t], n * KH)
            works = four("iw", "jw", lambda n: q.hw_s.at[t, n], lambda n: q.hw_r.at[t, n], lambda r: r.at[t])
            for c in works:
                c.start()
            if t == 0:
                for c in setups:
                    c.wait()
                for n in range(3):
                    open_up(q.js_fl, q.js_fr, n * KH, q.Hc, n * KJ)
            for c in works:
                c.wait()
            for n in range(2):
                open_up(q.jw_fl.at[t], q.jw_fr.at[t], n * KH, q.Hw.at[t], n * KJ)

        if final:
            def emit(g, carry):
                hvg = at(q.hv, pl.multiple_of(g * 8, 8))
                for j in range(GROUP):
                    uu, vv = pair(q.us, g, j), pair(q.vs, g, j)
                    r0, r1 = roll(uu[0], 1, 0), roll(uu[1], 1, 0)
                    edge = at(q.hu, 8 + g * 32 + 2 * j + 1, False)
                    put_pair(uo, g, j, (jnp.where(sub < 1, edge, r0), jnp.where(sub < 1, r0, r1)))
                    put_pair(vo, g, j, [
                        jnp.where(
                            lane == 0, roll(hvg, 125 - 4 * (2 * j + m), 1), roll(vv[m], 1, 1)
                        )
                        for m in range(2)
                    ])
                return carry

            each(emit, 0)
        for c in sends:
            c.wait()

        wb, pa = wb_own, pa_own
        for o in range(1, nz):
            d = lax.rem(me + o, nz)
            row = q.fgath[t, d]
            wb = wb + q.ctab[me * nz + d, 0:16, :] * row
            pa = pa + q.ctab[me * nz + d, 16:32, :] * row
        wb2, pa2 = halves(wb), halves(pa)

        if not final:
            fr, fl, iu, idn = (
                functools.reduce(lambda a, b: a + b, [ref[t, d] for d in range(nz)])
                for ref in (q.jc_fr, q.jc_fl, q.ic_up, q.ic_down)
            )
            halo_wp = spread(jnp.where(quad < 2, roll(fr, -2, 1), roll(fl, 2, 1)))
            own_wp = spread(pack_pair(wb, pa))
            for (ws, ps_), src, const, dst in (
                (halo_wp, q.Hw.at[t], q.Hc, q.Hp.at[t + 1]), (own_wp, q.Ow.at[t], q.Oc, q.Op.at[t])
            ):
                before = ws
                for k in range(0, KJ, 8):
                    star, w0 = src[k:k + 8, :], src[KJ + k:KJ + k + 8, :]
                    cs, cx, cy = (const[n * KJ + k:n * KJ + k + 8, :] for n in range(3))
                    now = roll(w0 + cx * ws + cy * ps_, 8, 1)
                    dst[k:k + 8, :] = star - cs * (
                        (w0 + cx * ws + cy * ps_) - jnp.where(lane < 8, before, now)
                    )
                    before = now

            def rows_of(v, src, const, dst):
                z = jnp.where(sub < 4, v, roll(v, 4, 0))
                r = roll(z, 2, 0)
                ws, ps_ = jnp.where(sub % 4 < 2, z, r), jnp.where(sub % 4 < 2, r, z)
                before = ws
                for k in range(0, K2, 8):
                    star, w0 = src[k:k + 8, :], src[K2 + k:K2 + k + 8, :]
                    cs, cx, cy = (const[n * K2 + k:n * K2 + k + 8, :] for n in range(3))
                    wn = w0 + cx * ws + cy * ps_
                    now = roll(wn, 2, 0)
                    dst[8 + k:16 + k, :] = star - cs * (wn - jnp.where(sub < 2, before, now))
                    before = now

            rows_of(iu, q.iw_up.at[t], q.is_up, q.p_up.at[t])
            rows_of(idn, q.iw_down.at[t], q.is_down, q.p_down.at[t])

        def implicit(g, wprev):
            for j in range(GROUP):
                w0, xx, yy = pair(w, g, j), pair(q.X, g, j), pair(q.Y, g, j)
                ss, star = pair(q.s, g, j), pair(q.ps, g, j)
                wn = tuple(w0[m] + xx[m] * wb2[m] + yy[m] * pa2[m] for m in range(2))
                pn = tuple(star[m] - ss[m] * (wn[m] - wprev[m]) for m in range(2))
                put_pair(w, g, j, wn)
                put_pair(p, g, j, pn)
                if not final:
                    edge_rows(g, j, pn, q.p_low.at[t], None, 8)
                wprev = wn
            return wprev

        each(implicit, wb2)


def store(u, v, w, p, u_out, v_out, w_out, p_out, sem):
    copies = [
        pltpu.make_async_copy(src, dst, sem.at[n])
        for n, (src, dst) in enumerate(((u, u_out), (v, v_out), (w, w_out), (p, p_out)))
    ]
    for c in copies:
        c.start()
    for c in copies:
        c.wait()


def solution(mesh):
    nx, ny, nz = (mesh.shape[a] for a in ("gx", "gy", "lev"))

    def shards(*fields):
        K, I, J = fields[0].shape
        assert I == 16 and J == 128 and K % (2 * GROUP) == 0
        R = K * I
        full = pltpu.VMEM((R, J), F32)
        held = scratch(K, J, nz)
        outs = pl.pallas_call(
            functools.partial(kernel, tuple(held), K, nx, ny, nz),
            out_shape=[full] * 4,
            in_specs=[pl.BlockSpec(memory_space=pl.ANY)] * 6,
            out_specs=[pl.BlockSpec(memory_space=pltpu.VMEM)] * 4,
            scratch_shapes=list(held.values()),
            compiler_params=pltpu.CompilerParams(collective_id=0, has_side_effects=True),
        )(*(f.reshape(R, J) for f in fields))
        outs = pl.pallas_call(
            store,
            out_shape=[jax.ShapeDtypeStruct((R, J), F32)] * 4,
            in_specs=[pl.BlockSpec(memory_space=pltpu.VMEM)] * 4,
            out_specs=[pl.BlockSpec(memory_space=pl.ANY)] * 4,
            scratch_shapes=[pltpu.SemaphoreType.DMA((4,))],
        )(*(pltpu.with_memory_space_constraint(o, pltpu.VMEM) for o in outs))
        return tuple(o.reshape(K, I, J) for o in outs)

    spec = P("lev", "gx", "gy")
    return jax.shard_map(
        shards, mesh=mesh, in_specs=(spec,) * 6, out_specs=(spec,) * 4, check_vma=False
    )
```

time: 35 us -> 33.5 us (0.957)
  Pallas kernels: 34.2 us -> 32.7 us
    pallas_call x1, Pallas kernels: 32.9 us -> 31.4 us  [shards(): pl.pallas_call(functools.partial(kernel, tuple(held), K, nx, ny, nz), out...]
where the time goes in v1:
time: 33.5 us; the launch traced here: 33.4 us
  Pallas kernels  32.7 us (98%)
  between operations  0.64 us (2%)
    pallas_call x1, Pallas kernels, shards(): pl.pallas_call(functools.partial(kernel, tuple(held), K, nx, ny, nz), out...  31.4 us
    pallas_call x1, Pallas kernels, shards(): pl.pallas_call(store, out_shape=[jax.ShapeDtypeStruct((R, J), F32)] * 4,...  1.35 us

profile of v1, /device:TPU:0, one launch (start us, length us, event | category | flops | bytes accessed | tf_op | source)
XLA Modules:
  0.0 33.4 jit_solution(9500285999170476732)
XLA Ops:
  0.6 31.4 %shard_map.93 = (f32[1024,128]{1,0:T(8,128)S(1)}, f32[1024,128]{1,0:T(8,128)S(1)}, f32[1024,128]{1,0:T(8,128)S(1)}, f32[1024,128]{1,0:T(8,128)S(1)}) custom-call(f32[1024,128]{1,0:T(8,128)} %bitcast.10, f32[1024,128]{1,0:T(8,128)} %bitcast.11, f32[1024,128]{1,0:T(8,128)} %bitcast.12, f32[1024,128]{1,0:T(8,128)} %bitcast.13, f32[1024,128]{1,0:T(8,128)} %bitcast.14, ...), custom_call_target="tpu_custom_call" | custom-call | tf_op jit(solution)/shard_map/pallas_call | solution.py:604
  32.0 1.3 %shard_map.94 = (f32[1024,128]{1,0:T(8,128)}, f32[1024,128]{1,0:T(8,128)}, f32[1024,128]{1,0:T(8,128)}, f32[1024,128]{1,0:T(8,128)}) custom-call(f32[1024,128]{1,0:T(8,128)S(1)} %get-tuple-element.12.u, f32[1024,128]{1,0:T(8,128)S(1)} %get-tuple-element.13.v, f32[1024,128]{1,0:T(8,128)S(1)} %get-tuple-element.14.w, f32[1024,128]{1,0:T(8,128)S(1)} %get-tuple-element.15.p), custom_call_target="tpu_custom_call" | custom-call | tf_op jit(solution)/shard_map/pallas_call | solution.py:612

commit v2 on v1

--- a/solution.py
+++ b/solution.py
@@ -21,7 +21,10 @@
     V = lambda *s: pltpu.VMEM((*s, J), F32)
     D = lambda *s: pltpu.SemaphoreType.DMA(s)
     m = max(nz - 1, 1)
-    s = {n: V(R) for n in ("us", "vs", "s", "bi", "bj", "E", "D", "H", "X", "Y", "ps", "h")}
+    s = {n: V(R) for n in (
+        "us", "vs", "s", "bi", "bj", "E", "D", "H", "X", "Y", "ps", "h",
+        "dX", "dY", "P", "Q", "XG", "YG",
+    )}
     s |= {n: V(3 * K2 + 16) for n in ("i0_low", "i0_high", "i0_up", "i0_down")}
     s |= {n: V(2 * KH) for n in ("j0_right", "j0_left", "j0_fl", "j0_fr")}
     s |= {n: V(3 * K2) for n in ("is_low", "is_high", "is_up", "is_down")}
@@ -30,11 +33,16 @@
     s |= {n: V(T, 2 * KH) for n in ("jw_right", "jw_left", "jw_fl", "jw_fr")}
     s |= {n: V(T, nz, 8) for n in ("ic_low", "ic_high", "ic_up", "ic_down", "jc", "jc_fl", "jc_fr")}
     s |= {n: V(T, K2 + 16) for n in ("p_up", "p_down", "p_low")}
+    s |= {n: V(T, K2) for n in ("b_up", "b_down", "b_low")}
+    s |= {n: V(K2) for n in ("bih",)}
+    s |= {n: V(2 * K2 + 16) for n in ("mi",)}
+    s |= {n: V(2 * KJ) for n in ("cj", "wo")}
+    s |= {"coef": V(19, 16)}
     s |= {n: V(3 * KJ) for n in ("own0",)}
     s |= {n: V(KJ) for n in ("hv", "hbj", "C", "vbr")}
     s |= {n: V(3 * KJ) for n in ("Hc", "Oc")}
     s |= {n: V(T, 2 * KJ) for n in ("Hw", "Ow")}
-    s |= {n: V(T, KJ) for n in ("Hp", "Op")}
+    s |= {n: V(T, KJ) for n in ("Hp", "Op", "Hb", "Ob")}
     s |= {n: V(K2 + 16) for n in ("hu", "hbi")}
     s |= {"cmine": V(64), "cgath": V(nz, 64), "fmine": V(T, 2, 16), "fgath": V(T, nz, 16)}
     s |= {"ctab": V(nz * nz, 32), "mine": V(80)}
@@ -216,9 +224,11 @@
                 e = hh * ss[m]
                 put(q.D, row, d)
                 put(q.H, row, hh)
+                od = o * d
                 put(q.E, row, e)
-                put(q.Y, row, hh * Z[m])
-                newB.append(ss[m] * (o * d))
+                put(q.Y, row, d * Z[m])
+                put(q.dX, row, od)
+                newB.append(ss[m] * od)
                 newZ.append(e * Z[m])
             B, Z = tuple(newB), tuple(newZ)
         return B, Z
@@ -229,12 +239,19 @@
         x, y = carry
         accs = [zero] * 3
         for j in range(GROUP):
-            ee, hz = pair(q.E, g, j), pair(q.Y, g, j)
-            x = tuple(ee[m] * x[m] for m in range(2))
-            y = tuple(ee[m] * y[m] - hz[m] for m in range(2))
-            put_pair(q.X, g, j, x)
-            put_pair(q.Y, g, j, y)
-            for n, val in enumerate((pair(q.s, g, j), x, y)):
+            bb, ss, dd = pair(q.bi, g, j), pair(q.s, g, j), pair(q.D, g, j)
+            od, dz = pair(q.dX, g, j), pair(q.Y, g, j)
+            vals = []
+            for m in range(2):
+                sd, gb = ss[m] * dd[m], GAIN * bb[m]
+                xg, yg = sd * x[m], sd * y[m] - dz[m]
+                dx, dy = -(od[m] * x[m]), -(od[m] * y[m] + gb * dz[m])
+                vals.append((gb * xg, gb * yg, xg, yg, dx, dy, ss[m] * dx, ss[m] * dy))
+            vals = list(zip(*vals))
+            x, y = vals[:2]
+            for ref, val in zip((q.X, q.Y, q.XG, q.YG, q.dX, q.dY, q.P, q.Q), vals):
+                put_pair(ref, g, j, val)
+            for n, val in enumerate((ss, vals[6], vals[7])):
                 edge_rows(g, j, val, q.is_low, q.is_high, n * K2)
                 accs[n] = pack_columns(j, val, accs[n])
         for n in range(3):
@@ -370,18 +387,241 @@
         r = roll(z, 8, 1)
         return jnp.where(lane % 16 < 8, z, r), jnp.where(lane % 16 < 8, r, z)
 
+    def insert(v, base):
+        return roll(v, 126 - base, 1)
+
+    def level_sums():
+        for k in range(0, K2, 8):
+            own, above = q.i0_high[pl.ds(9 + K2 + k, 8), :], q.i0_up[pl.ds(7 + K2 + k, 8), :]
+            q.bih[k:k + 8, :] = CH * jnp.where(sub % 2 == 0, own, above)
+            for n in range(2):
+                q.mi[n * K2 + k:n * K2 + k + 8, :] = (
+                    q.hbi[8 + k:16 + k, :] * q.is_down[(n + 1) * K2 + k:(n + 1) * K2 + k + 8, :]
+                )
+        for k in range(0, KJ, 8):
+            bjo = CH * jnp.where(quad == 0, roll(q.own0[KJ + k:KJ + k + 8, :], -1, 1), q.vbr[k:k + 8, :])
+            for n in range(2):
+                h, o = (r[(n + 1) * KJ + k:(n + 1) * KJ + k + 8, :] for r in (q.Hc, q.Oc))
+                q.cj[n * KJ + k:n * KJ + k + 8, :] = jnp.where(quad < 2, h, q.hbj[k:k + 8, :] * h)
+                q.wo[n * KJ + k:n * KJ + k + 8, :] = CH * jnp.where(quad < 2, o * bjo, o)
+
+        def add(acc, n, m, value):
+            acc[n][m] = acc[n][m] + value
+
+        def along_i(g, carry):
+            acc = [list(c) for c in carry]
+            for j in range(GROUP):
+                pq = (pair(q.P, g, j), pair(q.Q, g, j))
+                bb = pair(q.bi, g, j)
+                ahead, behind = [], []
+                for n, (g0, g1) in enumerate(pq):
+                    r0, r1 = roll(g0, 6, 0), roll(g1, 6, 0)
+                    edge = q.is_up[pl.ds((n + 1) * K2 + g * 32 + 2 * j - 6, 8), :]
+                    ahead.append((
+                        bb[0] * jnp.where(sub < 6, r0, r1), bb[1] * jnp.where(sub < 6, r1, edge)
+                    ))
+                    r0, r1 = roll(bb[0] * g0, 2, 0), roll(bb[1] * g1, 2, 0)
+                    edge = q.mi[pl.ds(n * K2 + g * 32 + 2 * j, 8), :]
+                    behind.append((jnp.where(sub < 2, edge, r0), jnp.where(sub < 2, r0, r1)))
+                for f in range(2):
+                    for m in range(2):
+                        cf = CH * pq[f][m]
+                        for n in range(2):
+                            add(acc, 2 * f + n, m, cf * ahead[n][m])
+                            add(acc, 4 + 2 * f + n, m, cf * behind[n][m])
+            return tuple(tuple(c) for c in acc)
+
+        def along_j(g, carry):
+            acc = [list(c) for c in carry]
+            cs = [at(q.cj, n * KJ + g * 8) for n in range(2)]
+            for j in range(GROUP):
+                pq = (pair(q.P, g, j), pair(q.Q, g, j))
+                bb = pair(q.bj, g, j)
+                for m in range(2):
+                    ahead, behind = [], []
+                    for n in range(2):
+                        edge = insert(cs[n], 4 * (2 * j + m))
+                        ahead.append(bb[m] * jnp.where(lane >= 126, edge, roll(pq[n][m], 126, 1)))
+                        behind.append(jnp.where(lane < 2, edge, roll(bb[m] * pq[n][m], 2, 1)))
+                    for f in range(2):
+                        cf = CH * pq[f][m]
+                        for n in range(2):
+                            add(acc, 2 * f + n, m, cf * ahead[n])
+                            add(acc, 4 + 2 * f + n, m, cf * behind[n])
+            return tuple(tuple(c) for c in acc)
+
+        def centre(g, carry):
+            acc = [list(c) for c in carry]
+            hb = at(q.hbj, g * 8)
+            for j in range(GROUP):
+                bbi, bbj = pair(q.bi, g, j), pair(q.bj, g, j)
+                pp, qq, dx, dy = (pair(r, g, j) for r in (q.P, q.Q, q.dX, q.dY))
+                xx, yy, xg, yg = (pair(r, g, j) for r in (q.X, q.Y, q.XG, q.YG))
+                r0, r1 = roll(bbi[0], 2, 0), roll(bbi[1], 2, 0)
+                edge = at(q.hbi, 8 + g * 32 + 2 * j, False)
+                bim = (jnp.where(sub < 2, edge, r0), jnp.where(sub < 2, r0, r1))
+                for m in range(2):
+                    bjm = jnp.where(lane < 2, insert(hb, 4 * (2 * j + m)), roll(bbj[m], 2, 1))
+                    sb = CH * ((bbi[m] + bim[m]) + (bbj[m] + bjm))
+                    fx, fy = dx[m] - sb * pp[m], dy[m] - sb * qq[m]
+                    add(acc, 0, m, pp[m] * fx - xg[m] * xx[m])
+                    add(acc, 1, m, qq[m] * fx - xg[m] * yy[m])
+                    add(acc, 2, m, qq[m] * fy - yg[m] * yy[m])
+            return tuple(tuple(c) for c in acc)
+
+        first = 0
+        for body, count in ((centre, 3), (along_i, 8), (along_j, 8)):
+            for n, val in enumerate(each(body, ((zero, zero),) * count)):
+                q.coef[first + n, 0:8, :], q.coef[first + n, 8:16, :] = val
+            first += count
+
+    def base_rows(t):
+        def body(g, carry):
+            A, W, before = carry
+            for j in range(GROUP):
+                star, w0, ss, uu, vv, bbi, bbj, dx, dy, pp, qq, xg, yg = (
+                    pair(r, g, j) for r in (
+                        q.ps, w, q.s, q.us, q.vs, q.bi, q.bj, q.dX, q.dY, q.P, q.Q, q.XG, q.YG
+                    )
+                )
+                pt = tuple(star[m] - ss[m] * (w0[m] - before[m]) for m in range(2))
+                r0, r1 = roll(pt[0], 6, 0), roll(pt[1], 6, 0)
+                pi = (jnp.where(sub < 6, r0, r1), jnp.where(sub < 6, r1, 0.0))
+                un = tuple(uu[m] - bbi[m] * (pi[m] - pt[m]) for m in range(2))
+                r0, r1 = roll(un[0], 2, 0), roll(un[1], 2, 0)
+                um = (jnp.where(sub < 2, 0.0, r0), jnp.where(sub < 2, r0, r1))
+                newA, newW = [], []
+                for m in range(2):
+                    pj = jnp.where(lane >= 126, 0.0, roll(pt[m], 126, 1))
+                    vn = vv[m] - bbj[m] * (pj - pt[m])
+                    vm = jnp.where(lane < 2, 0.0, roll(vn, 2, 1))
+                    div = CH * ((un[m] - um[m]) + (vn - vm))
+                    newA.append(A[m] + (pp[m] * div - (dx[m] * pt[m] + xg[m] * w0[m])))
+                    newW.append(W[m] + (qq[m] * div - (dy[m] * pt[m] + yg[m] * w0[m])))
+                A, W, before = tuple(newA), tuple(newW), w0
+            return A, W, before
+
+        A, W, _ = each(body, ((zero, zero),) * 3)
+        return list(A), list(W)
+
+    def rows_without(src, const, dst):
+        before = zero
+        for k in range(0, K2, 8):
+            star, w0, cs = src[k:k + 8, :], src[K2 + k:K2 + k + 8, :], const[k:k + 8, :]
+            now = roll(w0, 2, 0)
+            dst[k:k + 8, :] = star - cs * (w0 - jnp.where(sub < 2, before, now))
+            before = now
+
+    def columns_without(src, const, dst):
+        before = zero
+        for k in range(0, KJ, 8):
+            star, w0, cs = src[k:k + 8, :], src[KJ + k:KJ + k + 8, :], const[k:k + 8, :]
+            now = roll(w0, 8, 1)
+            dst[k:k + 8, :] = star - cs * (w0 - jnp.where(lane < 8, before, now))
+            before = now
+
+    def halo_rows(t, A, W):
+        lows, highs, cols = [zero, zero], [zero, zero], [zero, zero]
+        for k in range(0, K2, 8):
+            hu_new = q.hu[8 + k:16 + k, :] - q.hbi[8 + k:16 + k, :] * (
+                q.b_low[t, k:k + 8, :] - q.b_down[t, k:k + 8, :]
+            )
+            high = q.bih[k:k + 8, :] * q.b_up[t, k:k + 8, :]
+            for n in range(2):
+                r = (n + 1) * K2 + k
+                lows[n] = lows[n] + q.is_low[r:r + 8, :] * hu_new
+                highs[n] = highs[n] + q.is_high[r:r + 8, :] * high
+        for k in range(0, KJ, 8):
+            hp = q.Hb[t, k:k + 8, :]
+            c = jnp.where(
+                quad < 2, hp, q.hv[k:k + 8, :] - q.hbj[k:k + 8, :] * (q.Ob[t, k:k + 8, :] - hp)
+            )
+            for n in range(2):
+                cols[n] = cols[n] + q.wo[n * KJ + k:n * KJ + k + 8, :] * c
+        for n, rows in enumerate((A, W)):
+            low, high, col = lows[n], highs[n], cols[n]
+            for r in (4, 2):
+                low, high = low + roll(low, r, 0), high + roll(high, r, 0)
+            for r in (64, 32, 16, 8):
+                col = col + roll(col, r, 1)
+            rows[0] = rows[0] - jnp.where(sub < 2, CH * low, 0.0)
+            rows[1] = rows[1] - jnp.where(sub >= 6, CH * high, 0.0)
+            for m in range(2):
+                rows[m] = rows[m] - jnp.where((lane >= 126) | (lane < 2), insert(col, 4 * m), 0.0)
+
+    def send_round(t, W0, A0):
+        final = t == SUBSTEPS - 1
+        wa, aw, r2psi, br, brx = (q.mine[16 * n:16 * n + 16, :] for n in range(5))
+        up_row, down_row = W0 + wa * A0, A0 + aw * W0
+        q.fmine[t, 0], q.fmine[t, 1] = up_row, down_row
+        sends = []
+        wb_own = r2psi * down_row
+        pa_own = br * W0 + brx * wb_own
+        for o in sorted(range(nz), key=lambda o: -min(o, nz - o)):
+            L = lax.rem(me + o, nz)
+            if not final:
+                if o:
+                    row = jnp.where(L > me, up_row, down_row)
+                    wc, pc = (q.ctab[L * nz + me, 16 * n:16 * n + 16, :] * row for n in range(2))
+                else:
+                    wc, pc = wb_own, pa_own
+                q.jc[t, o] = pack_pair(wc, pc)
+                q.ic_low[t, o] = jnp.where(sub < 2, wc[0:8], roll(pc[0:8], 2, 0))
+                q.ic_high[t, o] = jnp.where(sub < 2, roll(wc[8:16], 2, 0), roll(pc[8:16], 4, 0))
+                for n, (a, b) in enumerate((
+                    (q.jc, q.jc_fl), (q.jc, q.jc_fr), (q.ic_low, q.ic_up), (q.ic_high, q.ic_down)
+                )):
+                    c = remote(
+                        a.at[t, o], b.at[t, me], q.hc_s.at[t, n, o], q.hc_r.at[t, n, o],
+                        {**sides[n], "lev": L},
+                    )
+                    c.start()
+                    sends.append(c)
+            if o:
+                c = remote(
+                    q.fmine.at[t, lax.div(me + o, nz)], q.fgath.at[t, me],
+                    q.ls_s.at[t, o - 1], q.ls_r.at[t, o - 1], {"lev": L},
+                )
+                c.start()
+                sends.append(c)
+        return sends, wb_own, pa_own
+
     for t in range(SUBSTEPS):
         final = t == SUBSTEPS - 1
+        if t:
+            each(implicit, wb2)
+
+            def add_columns(src, const, wp, dst):
+                for k in range(0, KJ, 8):
+                    dst[k:k + 8, :] = src[k:k + 8, :] - (
+                        const[KJ + k:KJ + k + 8, :] * wp[0] + const[2 * KJ + k:2 * KJ + k + 8, :] * wp[1]
+                    )
+
+            def add_rows(src, const, v, dst):
+                z = jnp.where(sub < 4, v, roll(v, 4, 0))
+                r = roll(z, 2, 0)
+                ws, ps_ = jnp.where(sub % 4 < 2, z, r), jnp.where(sub % 4 < 2, r, z)
+                for k in range(0, K2, 8):
+                    dst[8 + k:16 + k, :] = src[k:k + 8, :] - (
+                        const[K2 + k:K2 + k + 8, :] * ws + const[2 * K2 + k:2 * K2 + k + 8, :] * ps_
+                    )
+
+            add_columns(q.Hb.at[t - 1], q.Hc, spread(halo_j), q.Hp.at[t])
+            add_columns(q.Ob.at[t - 1], q.Oc, spread(pack_pair(wb, pa)), q.Op.at[t])
+            low = jnp.where(sub < 2, wb[0:8], roll(pa[0:8], 2, 0))
+            add_rows(q.b_up.at[t - 1], q.is_up, halo_up, q.p_up.at[t])
+            add_rows(q.b_down.at[t - 1], q.is_down, halo_down, q.p_down.at[t])
+            add_rows(q.b_low.at[t - 1], q.is_low, low, q.p_low.at[t])
         i_up, i_down, i_low = (
             (q.i0_up, q.i0_down, q.i0_low) if t == 0
-            else (q.p_up.at[t - 1], q.p_down.at[t - 1], q.p_low.at[t - 1])
+            else (q.p_up.at[t], q.p_down.at[t], q.p_low.at[t])
         )
-        own_p, own_base = (q.own0, 0) if t == 0 else (q.Op.at[t - 1], 0)
+        own_p = q.own0 if t == 0 else q.Op.at[t]
         halo_p = q.Hp.at[t]
 
         for k in range(0, KJ, 8):
             hp = halo_p[k:k + 8, :]
-            hv_new = q.hv[k:k + 8, :] - q.hbj[k:k + 8, :] * (own_p[own_base + k:own_base + k + 8, :] - hp)
+            hv_new = q.hv[k:k + 8, :] - q.hbj[k:k + 8, :] * (own_p[k:k + 8, :] - hp)
             q.hv[k:k + 8, :] = hv_new
             q.C[k:k + 8, :] = jnp.where(quad < 2, hp, hv_new)
 
@@ -448,58 +688,31 @@
             for c in consts:
                 c.wait()
             interface()
-
-        wa, aw, r2psi, br, brx = (q.mine[16 * n:16 * n + 16, :] for n in range(5))
-        A0, W0 = (jnp.concatenate(n, 0) for n in (A, x))
-        up_row, down_row = W0 + wa * A0, A0 + aw * W0
-        q.fmine[t, 0], q.fmine[t, 1] = up_row, down_row
-        sends, peers = [], {}
-        for o in range(1, nz):
-            peers[o] = remote(
-                q.fmine.at[t, lax.div(me + o, nz)], q.fgath.at[t, me],
-                q.ls_s.at[t, o - 1], q.ls_r.at[t, o - 1], {"lev": lax.rem(me + o, nz)},
-            )
-        wb_own = r2psi * down_row
-        pa_own = br * W0 + brx * wb_own
-        order = sorted(range(nz), key=lambda o: -min(o, nz - o))
-        for o in order:
-            if not final:
-                L = lax.rem(me + o, nz)
-                if o:
-                    row = q.fmine[t, lax.div(me + o, nz)]
-                    wc, pc = (q.ctab[L * nz + me, 16 * n:16 * n + 16, :] * row for n in range(2))
-                else:
-                    wc, pc = wb_own, pa_own
-                q.jc[t, o] = pack_pair(wc, pc)
-                q.ic_low[t, o] = jnp.where(sub < 2, wc[0:8], roll(pc[0:8], 2, 0))
-                q.ic_high[t, o] = jnp.where(sub < 2, roll(wc[8:16], 2, 0), roll(pc[8:16], 4, 0))
-                for n, (a, b) in enumerate((
-                    (q.jc, q.jc_fl), (q.jc, q.jc_fr), (q.ic_low, q.ic_up), (q.ic_high, q.ic_down)
-                )):
-                    c = remote(
-                        a.at[t, o], b.at[t, me], q.hc_s.at[t, n, o], q.hc_r.at[t, n, o],
-                        {**sides[n], "lev": L},
-                    )
-                    c.start()
-                    sends.append(c)
-            if o:
-                peers[o].start()
-                sends.append(peers[o])
+            A0, W0 = (jnp.concatenate(n, 0) for n in (A, x))
+            sends, wb_own, pa_own = send_round(0, W0, A0)
         if not final:
             for n in range(2):
                 dense(q.Ow.at[t], n * KJ, q.jw_right.at[t], q.jw_left.at[t], n * KH)
             works = four("iw", "jw", lambda n: q.hw_s.at[t, n], lambda n: q.hw_r.at[t, n], lambda r: r.at[t])
             for c in works:
                 c.start()
+            A1, W1 = base_rows(t)
             if t == 0:
                 for c in setups:
                     c.wait()
                 for n in range(3):
                     open_up(q.js_fl, q.js_fr, n * KH, q.Hc, n * KJ)
+                level_sums()
+            columns_without(q.Ow.at[t], q.Oc, q.Ob.at[t])
+            rows_without(q.iw_low.at[t], q.is_low, q.b_low.at[t])
             for c in works:
                 c.wait()
             for n in range(2):
                 open_up(q.jw_fl.at[t], q.jw_fr.at[t], n * KH, q.Hw.at[t], n * KJ)
+            columns_without(q.Hw.at[t], q.Hc, q.Hb.at[t])
+            rows_without(q.iw_up.at[t], q.is_up, q.b_up.at[t])
+            rows_without(q.iw_down.at[t], q.is_down, q.b_down.at[t])
+            halo_rows(t, A1, W1)
 
         if final:
             def emit(g, carry):
@@ -530,42 +743,41 @@
         wb2, pa2 = halves(wb), halves(pa)
 
         if not final:
-            fr, fl, iu, idn = (
+            fr, fl, halo_up, halo_down = (
                 functools.reduce(lambda a, b: a + b, [ref[t, d] for d in range(nz)])
                 for ref in (q.jc_fr, q.jc_fl, q.ic_up, q.ic_down)
             )
-            halo_wp = spread(jnp.where(quad < 2, roll(fr, -2, 1), roll(fl, 2, 1)))
-            own_wp = spread(pack_pair(wb, pa))
-            for (ws, ps_), src, const, dst in (
-                (halo_wp, q.Hw.at[t], q.Hc, q.Hp.at[t + 1]), (own_wp, q.Ow.at[t], q.Oc, q.Op.at[t])
-            ):
-                before = ws
-                for k in range(0, KJ, 8):
-                    star, w0 = src[k:k + 8, :], src[KJ + k:KJ + k + 8, :]
-                    cs, cx, cy = (const[n * KJ + k:n * KJ + k + 8, :] for n in range(3))
-                    now = roll(w0 + cx * ws + cy * ps_, 8, 1)
-                    dst[k:k + 8, :] = star - cs * (
-                        (w0 + cx * ws + cy * ps_) - jnp.where(lane < 8, before, now)
-                    )
-                    before = now
-
-            def rows_of(v, src, const, dst):
-                z = jnp.where(sub < 4, v, roll(v, 4, 0))
-                r = roll(z, 2, 0)
-                ws, ps_ = jnp.where(sub % 4 < 2, z, r), jnp.where(sub % 4 < 2, r, z)
-                before = ws
-                for k in range(0, K2, 8):
-                    star, w0 = src[k:k + 8, :], src[K2 + k:K2 + k + 8, :]
-                    cs, cx, cy = (const[n * K2 + k:n * K2 + k + 8, :] for n in range(3))
-                    wn = w0 + cx * ws + cy * ps_
-                    now = roll(wn, 2, 0)
-                    dst[8 + k:16 + k, :] = star - cs * (wn - jnp.where(sub < 2, before, now))
-                    before = now
-
-            rows_of(iu, q.iw_up.at[t], q.is_up, q.p_up.at[t])
-            rows_of(idn, q.iw_down.at[t], q.is_down, q.p_down.at[t])
-
-        def implicit(g, wprev):
+            halo_j = jnp.where(quad < 2, roll(fr, -2, 1), roll(fl, 2, 1))
+            stencil = []
+            for n, v in enumerate((wb2, pa2)):
+                a0, a1, b0, b1 = (roll(v[m], k, 0) for k in (6, 2) for m in range(2))
+                above, below = roll(halo_up, 6 - 2 * n, 0), roll(halo_down, -2 * n, 0)
+                edges = [insert(halo_j, 8 * n + 4 * m) for m in range(2)]
+                stencil.append((
+                    v,
+                    (jnp.where(sub < 6, a0, a1), jnp.where(sub < 6, a1, above)),
+                    (jnp.where(sub < 2, below, b0), jnp.where(sub < 2, b0, b1)),
+                    tuple(jnp.where(lane >= 126, edges[m], roll(v[m], 126, 1)) for m in range(2)),
+                    tuple(jnp.where(lane < 2, edges[m], roll(v[m], 2, 1)) for m in range(2)),
+                ))
+            rows = []
+            for f, base in enumerate((A1, W1)):
+                halves_ = []
+                for m in range(2):
+                    terms = [base[m]]
+                    for n in range(2):
+                        for k in range(5):
+                            c = f + n if k == 0 else 3 + 4 * (k - 1) + 2 * f + n
+                            terms.append(q.coef[c, 8 * m:8 * m + 8, :] * stencil[n][k][m])
+                    while len(terms) > 1:
+                        terms = [
+                            sum(terms[k + 1:k + 2], terms[k]) for k in range(0, len(terms), 2)
+                        ]
+                    halves_.append(terms[0])
+                rows.append(jnp.concatenate(halves_, 0))
+            sends, wb_own, pa_own = send_round(t + 1, rows[1], rows[0])
+
+        def implicit(g, wprev, wb2=wb2, pa2=pa2):
             for j in range(GROUP):
                 w0, xx, yy = pair(w, g, j), pair(q.X, g, j), pair(q.Y, g, j)
                 ss, star = pair(q.s, g, j), pair(q.ps, g, j)
@@ -573,12 +785,10 @@
                 pn = tuple(star[m] - ss[m] * (wn[m] - wprev[m]) for m in range(2))
                 put_pair(w, g, j, wn)
                 put_pair(p, g, j, pn)
-                if not final:
-                    edge_rows(g, j, pn, q.p_low.at[t], None, 8)
                 wprev = wn
             return wprev
 
-        each(implicit, wb2)
+    each(implicit, wb2)
 
 
 def store(u, v, w, p, u_out, v_out, w_out, p_out, sem):

time: 33.5 us -> 30.9 us (0.922)
  Pallas kernels: 32.7 us -> 30.1 us
    pallas_call x1, Pallas kernels: 31.4 us -> 28.7 us  [shards(): pl.pallas_call(functools.partial(kernel, tuple(held), K, nx, ny, nz), out...]
where the time goes in v2:
time: 30.9 us; the launch traced here: 30.7 us
  Pallas kernels  30.1 us (97%)
  between operations  0.64 us (2%)
    pallas_call x1, Pallas kernels, shards(): pl.pallas_call(functools.partial(kernel, tuple(held), K, nx, ny, nz), out...  28.7 us
    pallas_call x1, Pallas kernels, shards(): pl.pallas_call(store, out_shape=[jax.ShapeDtypeStruct((R, J), F32)] * 4,...  1.35 us

profile of v2, /device:TPU:0, one launch (start us, length us, event | category | flops | bytes accessed | tf_op | source)
XLA Modules:
  0.0 30.7 jit_solution(17303516979895505534)
XLA Ops:
  0.6 28.7 %shard_map.93 = (f32[1024,128]{1,0:T(8,128)S(1)}, f32[1024,128]{1,0:T(8,128)S(1)}, f32[1024,128]{1,0:T(8,128)S(1)}, f32[1024,128]{1,0:T(8,128)S(1)}) custom-call(f32[1024,128]{1,0:T(8,128)} %bitcast.10, f32[1024,128]{1,0:T(8,128)} %bitcast.11, f32[1024,128]{1,0:T(8,128)} %bitcast.12, f32[1024,128]{1,0:T(8,128)} %bitcast.13, f32[1024,128]{1,0:T(8,128)} %bitcast.14, ...), custom_call_target="tpu_custom_call" | custom-call | tf_op jit(solution)/shard_map/pallas_call | solution.py:814
  29.4 1.3 %shard_map.94 = (f32[1024,128]{1,0:T(8,128)}, f32[1024,128]{1,0:T(8,128)}, f32[1024,128]{1,0:T(8,128)}, f32[1024,128]{1,0:T(8,128)}) custom-call(f32[1024,128]{1,0:T(8,128)S(1)} %get-tuple-element.12.u, f32[1024,128]{1,0:T(8,128)S(1)} %get-tuple-element.13.v, f32[1024,128]{1,0:T(8,128)S(1)} %get-tuple-element.14.w, f32[1024,128]{1,0:T(8,128)S(1)} %get-tuple-element.15.p), custom_call_target="tpu_custom_call" | custom-call | tf_op jit(solution)/shard_map/pallas_call | solution.py:822

commit v3 on v2

--- a/solution.py
+++ b/solution.py
@@ -39,12 +39,12 @@
     s |= {n: V(2 * KJ) for n in ("cj", "wo")}
     s |= {"coef": V(19, 16)}
     s |= {n: V(3 * KJ) for n in ("own0",)}
-    s |= {n: V(KJ) for n in ("hv", "hbj", "C", "vbr")}
+    s |= {n: V(KJ) for n in ("hv", "hbj")}
     s |= {n: V(3 * KJ) for n in ("Hc", "Oc")}
     s |= {n: V(T, 2 * KJ) for n in ("Hw", "Ow")}
     s |= {n: V(T, KJ) for n in ("Hp", "Op", "Hb", "Ob")}
     s |= {n: V(K2 + 16) for n in ("hu", "hbi")}
-    s |= {"cmine": V(64), "cgath": V(nz, 64), "fmine": V(T, 2, 16), "fgath": V(T, nz, 16)}
+    s |= {"cmine": V(48), "cgath": V(nz, 48), "fmine": V(T, 2, 16), "fgath": V(T, nz, 16)}
     s |= {"ctab": V(nz * nz, 32), "mine": V(80)}
     s |= {"in_sem": D(6)}
     for n in ("h0", "hs"):
@@ -65,7 +65,7 @@
 
     loads = []
     for n, (src, dst) in enumerate(
-        ((p_in, p), (b_in, q.bi), (u_in, q.us), (v_in, q.vs), (s_in, q.s), (w_in, w))
+        ((p_in, p), (b_in, q.bi), (v_in, q.vs), (s_in, q.s), (u_in, q.us), (w_in, w))
     ):
         c = pltpu.make_async_copy(src, dst, q.in_sem.at[n])
         c.start()
@@ -140,19 +140,14 @@
                     quad < 2, roll(b, -2 * m, 1), roll(a, 2, 1) if m == 0 else a
                 )
 
-    for c in loads[:4]:
+    for c in loads[:3]:
         c.wait()
 
     def first_pack(g, carry):
         accp = accb = accv = zero
         for j in range(GROUP):
-            for n, ref in enumerate((p, q.bi, q.us)):
-                x = pair(ref, g, j)
-                edge_rows(g, j, x, q.i0_low, q.i0_high, 8 + n * K2)
-                if n == 0:
-                    accp = pack_columns(j, x, accp)
-                if n == 1:
-                    accb = pack_columns(j, x, accb)
+            accp = pack_columns(j, pair(p, g, j), accp)
+            accb = pack_columns(j, pair(q.bi, g, j), accb)
             accv = pack_columns(j, pair(q.vs, g, j), accv)
         put(q.own0, g * 8, accp)
         put(q.own0, KJ + g * 8, accb)
@@ -176,14 +171,6 @@
 
     pl.semaphore_wait(barrier, 4 + nz - 1)
 
-    def exchange(name, ss, rs, at_=lambda r: r):
-        return [
-            remote(at_(getattr(q, name + a)), at_(getattr(q, name + b)), ss(n), rs(n), dev)
-            for n, (a, b, dev) in enumerate(zip(
-                ("_right", "_left", "_low", "_high"), ("_fl", "_fr", "_up", "_down"), sides
-            ))
-        ]
-
     def four(i, j, ss, rs, at_=lambda r: r):
         pairs = (
             (j + "_right", j + "_fl"), (j + "_left", j + "_fr"),
@@ -205,16 +192,28 @@
             (q.j0_fl, q.j0_fr, q.i0_up, q.i0_down), sides,
         ))
     ]
-    for c in halos:
+    for c in halos[:2]:
         c.start()
 
     loads[4].wait()
 
+    def first_rows(g, carry):
+        for j in range(GROUP):
+            for n, ref in enumerate((p, q.bi, q.us)):
+                edge_rows(g, j, pair(ref, g, j), q.i0_low, q.i0_high, 8 + n * K2)
+        return carry
+
+    each(first_rows, 0)
+    for c in halos[2:]:
+        c.start()
+
+    loads[3].wait()
+
     def factor(g, carry):
-        B, Z = carry
+        B, Z, yend = carry
         for j in reversed(range(GROUP)):
             bb, ss = pair(q.bi, g, j), pair(q.s, g, j)
-            newB, newZ = [], []
+            newB, newZ, newy = [], [], []
             for m in range(2):
                 row = g * 256 + 16 * j + 8 * m
                 gb = GAIN * bb[m]
@@ -226,14 +225,26 @@
                 put(q.H, row, hh)
                 od = o * d
                 put(q.E, row, e)
-                put(q.Y, row, d * Z[m])
+                dz = d * Z[m]
+                put(q.Y, row, dz)
                 put(q.dX, row, od)
                 newB.append(ss[m] * od)
                 newZ.append(e * Z[m])
-            B, Z = tuple(newB), tuple(newZ)
-        return B, Z
-
-    B, Z = each(factor, ((zero, zero), (one, one)), downward=True)
+                newy.append(yend[m] - (gb * dz) * Z[m])
+            B, Z, yend = tuple(newB), tuple(newZ), tuple(newy)
+        return B, Z, yend
+
+    B, Z, yend = each(factor, ((zero, zero), (one, one), (zero, zero)), downward=True)
+    for n, val in enumerate((Z, yend, B)):
+        for m in range(2):
+            q.cmine[16 * n + 8 * m:16 * n + 8 * m + 8, :] = val[m]
+            q.cgath[me, 16 * n + 8 * m:16 * n + 8 * m + 8, :] = val[m]
+    consts = [
+        remote(q.cmine, q.cgath.at[me], q.cs_s.at[o - 1], q.cs_r.at[o - 1], {"lev": lax.rem(me + o, nz)})
+        for o in range(1, nz)
+    ]
+    for c in consts:
+        c.start()
 
     def responses(g, carry):
         x, y = carry
@@ -258,17 +269,7 @@
             put(q.Oc, n * KJ + g * 8, accs[n])
         return x, y
 
-    x, y = each(responses, ((one, one), (zero, zero)))
-    for n, val in enumerate((x, y, Z, B)):
-        for m in range(2):
-            q.cmine[16 * n + 8 * m:16 * n + 8 * m + 8, :] = val[m]
-            q.cgath[me, 16 * n + 8 * m:16 * n + 8 * m + 8, :] = val[m]
-    consts = [
-        remote(q.cmine, q.cgath.at[me], q.cs_s.at[o - 1], q.cs_r.at[o - 1], {"lev": lax.rem(me + o, nz)})
-        for o in range(1, nz)
-    ]
-    for c in consts:
-        c.start()
+    each(responses, ((one, one), (zero, zero)))
     for n in range(3):
         dense(q.Oc, n * KJ, q.js_right, q.js_left, n * KH)
     setups = four("is", "js", lambda n: q.hs_s.at[n], lambda n: q.hs_r.at[n])
@@ -276,8 +277,23 @@
         c.start()
 
     def crow(d, n):
+        n = (0, 1, 0, 2)[n]
         return q.cgath[d, 16 * n:16 * n + 16, :]
 
+    def stagger(g, carry):
+        for j in range(GROUP):
+            xb, xu, xv = pair(q.bi, g, j), pair(q.us, g, j), pair(q.vs, g, j)
+            xb = tuple(CH * v for v in xb)
+            for val, dst in ((xu, q.us), (xb, q.bi)):
+                r0, r1 = roll(val[0], 7, 0), roll(val[1], 7, 0)
+                put_pair(dst, g, j, (jnp.where(sub < 7, r0, r1), r1))
+            for val, dst in ((xv, q.vs), (xb, q.bj)):
+                put_pair(dst, g, j, [roll(v, 127, 1) for v in val])
+        return carry
+
+    each(stagger, 0)
+
+    loads[5].wait()
     for c in halos:
         c.wait()
 
@@ -286,32 +302,22 @@
         fl = q.j0_fl[KH + 8 * n:KH + 8 * n + 8, :]
         for m in range(2):
             k = 16 * n + 8 * m
-            q.vbr[k:k + 8, :] = roll(fr, -2 * m, 1)
-            flg = roll(fl, -2 * m, 1)
+            frg, flg = roll(fr, -2 * m, 1), roll(fl, -2 * m, 1)
             ab = q.own0[KJ + k:KJ + k + 8, :]
             av = q.own0[2 * KJ + k:2 * KJ + k + 8, :]
-            q.hv[k:k + 8, :] = jnp.where(quad == 2, roll(flg, 2, 1), roll(av, 1, 1))
-            q.hbj[k:k + 8, :] = CH * roll(jnp.where(quad == 1, flg, ab), 1, 1)
+            vright = jnp.where(quad == 0, roll(av, -1, 1), roll(frg, 1, 1))
+            bright = jnp.where(quad == 0, roll(ab, -1, 1), frg)
+            vleft = jnp.where(quad == 2, roll(flg, 2, 1), roll(av, 1, 1))
+            bleft = roll(jnp.where(quad == 1, flg, ab), 1, 1)
+            q.hv[k:k + 8, :] = jnp.where(quad < 2, vright, vleft)
+            q.hbj[k:k + 8, :] = CH * jnp.where(quad < 2, -bright, bleft)
     open_up(q.j0_fl, q.j0_fr, 0, q.Hp.at[0], 0)
 
-    def stagger(g, carry):
-        packed = at(q.vbr, g * 8)
+    def patch(g, carry):
         for j in range(GROUP):
-            xb, xu, xv = pair(q.bi, g, j), pair(q.us, g, j), pair(q.vs, g, j)
-            for (val, dst, scale, f) in ((xu, q.us, 1.0, 2), (xb, q.bi, CH, 1)):
-                r0, r1 = roll(val[0], 7, 0), roll(val[1], 7, 0)
-                edge = q.i0_up[pl.ds(8 + f * K2 + g * 32 + 2 * j - 7, 8), :]
-                put_pair(dst, g, j, (
-                    scale * jnp.where(sub < 7, r0, r1), scale * jnp.where(sub < 7, r1, edge)
-                ))
-            for (val, dst, scale, first) in ((xv, q.vs, 1.0, 127), (xb, q.bj, CH, 126)):
-                out = []
-                for m in range(2):
-                    n = 2 * j + m
-                    out.append(scale * jnp.where(
-                        lane == 127, roll(packed, first - 4 * n, 1), roll(val[m], 127, 1)
-                    ))
-                put_pair(dst, g, j, out)
+            row = g * 256 + 16 * j + 15
+            q.us[pl.ds(row, 1), :] = q.i0_up[pl.ds(8 + 2 * K2 + g * 32 + 2 * j, 1), :]
+            q.bi[pl.ds(row, 1), :] = CH * q.i0_up[pl.ds(8 + K2 + g * 32 + 2 * j, 1), :]
         for r in range(4):
             row = g * 32 + 8 * r
             for (dst, f, scale) in ((q.hu, 2, 1.0), (q.hbi, 1, CH)):
@@ -321,9 +327,7 @@
                 put(dst, 8 + row, scale * jnp.where(sub % 2 == 0, below, own))
         return carry
 
-    each(stagger, 0)
-
-    loads[5].wait()
+    each(patch, 0)
 
     def interface():
         beta = jnp.zeros((16, 128), F32)
@@ -399,11 +403,11 @@
                     q.hbi[8 + k:16 + k, :] * q.is_down[(n + 1) * K2 + k:(n + 1) * K2 + k + 8, :]
                 )
         for k in range(0, KJ, 8):
-            bjo = CH * jnp.where(quad == 0, roll(q.own0[KJ + k:KJ + k + 8, :], -1, 1), q.vbr[k:k + 8, :])
+            hb = q.hbj[k:k + 8, :]
             for n in range(2):
                 h, o = (r[(n + 1) * KJ + k:(n + 1) * KJ + k + 8, :] for r in (q.Hc, q.Oc))
-                q.cj[n * KJ + k:n * KJ + k + 8, :] = jnp.where(quad < 2, h, q.hbj[k:k + 8, :] * h)
-                q.wo[n * KJ + k:n * KJ + k + 8, :] = CH * jnp.where(quad < 2, o * bjo, o)
+                q.cj[n * KJ + k:n * KJ + k + 8, :] = jnp.where(quad < 2, -hb, hb) * h
+                q.wo[n * KJ + k:n * KJ + k + 8, :] = CH * jnp.where(quad < 2, -o, o)
 
         def add(acc, n, m, value):
             acc[n][m] = acc[n][m] + value
@@ -441,7 +445,7 @@
                     ahead, behind = [], []
                     for n in range(2):
                         edge = insert(cs[n], 4 * (2 * j + m))
-                        ahead.append(bb[m] * jnp.where(lane >= 126, edge, roll(pq[n][m], 126, 1)))
+                        ahead.append(jnp.where(lane >= 126, edge, bb[m] * roll(pq[n][m], 126, 1)))
                         behind.append(jnp.where(lane < 2, edge, roll(bb[m] * pq[n][m], 2, 1)))
                     for f in range(2):
                         cf = CH * pq[f][m]
@@ -453,6 +457,7 @@
         def centre(g, carry):
             acc = [list(c) for c in carry]
             hb = at(q.hbj, g * 8)
+            hb = jnp.where(quad < 2, -hb, hb)
             for j in range(GROUP):
                 bbi, bbj = pair(q.bi, g, j), pair(q.bj, g, j)
                 pp, qq, dx, dy = (pair(r, g, j) for r in (q.P, q.Q, q.dX, q.dY))
@@ -461,8 +466,9 @@
                 edge = at(q.hbi, 8 + g * 32 + 2 * j, False)
                 bim = (jnp.where(sub < 2, edge, r0), jnp.where(sub < 2, r0, r1))
                 for m in range(2):
-                    bjm = jnp.where(lane < 2, insert(hb, 4 * (2 * j + m)), roll(bbj[m], 2, 1))
-                    sb = CH * ((bbi[m] + bim[m]) + (bbj[m] + bjm))
+                    edge = insert(hb, 4 * (2 * j + m))
+                    bjm = jnp.where(lane < 2, edge, roll(bbj[m], 2, 1))
+                    sb = CH * ((bbi[m] + bim[m]) + (jnp.where(lane >= 126, edge, bbj[m]) + bjm))
                     fx, fy = dx[m] - sb * pp[m], dy[m] - sb * qq[m]
                     add(acc, 0, m, pp[m] * fx - xg[m] * xx[m])
                     add(acc, 1, m, qq[m] * fx - xg[m] * yy[m])
@@ -492,8 +498,8 @@
                 um = (jnp.where(sub < 2, 0.0, r0), jnp.where(sub < 2, r0, r1))
                 newA, newW = [], []
                 for m in range(2):
-                    pj = jnp.where(lane >= 126, 0.0, roll(pt[m], 126, 1))
-                    vn = vv[m] - bbj[m] * (pj - pt[m])
+                    vn = vv[m] - bbj[m] * (roll(pt[m], 126, 1) - pt[m])
+                    vn = jnp.where(lane >= 126, 0.0, vn)
                     vm = jnp.where(lane < 2, 0.0, roll(vn, 2, 1))
                     div = CH * ((un[m] - um[m]) + (vn - vm))
                     newA.append(A[m] + (pp[m] * div - (dx[m] * pt[m] + xg[m] * w0[m])))
@@ -532,10 +538,7 @@
                 lows[n] = lows[n] + q.is_low[r:r + 8, :] * hu_new
                 highs[n] = highs[n] + q.is_high[r:r + 8, :] * high
         for k in range(0, KJ, 8):
-            hp = q.Hb[t, k:k + 8, :]
-            c = jnp.where(
-                quad < 2, hp, q.hv[k:k + 8, :] - q.hbj[k:k + 8, :] * (q.Ob[t, k:k + 8, :] - hp)
-            )
+            c = q.hv[k:k + 8, :] - q.hbj[k:k + 8, :] * (q.Ob[t, k:k + 8, :] - q.Hb[t, k:k + 8, :])
             for n in range(2):
                 cols[n] = cols[n] + q.wo[n * KJ + k:n * KJ + k + 8, :] * c
         for n, rows in enumerate((A, W)):
@@ -620,10 +623,9 @@
         halo_p = q.Hp.at[t]
 
         for k in range(0, KJ, 8):
-            hp = halo_p[k:k + 8, :]
-            hv_new = q.hv[k:k + 8, :] - q.hbj[k:k + 8, :] * (own_p[k:k + 8, :] - hp)
-            q.hv[k:k + 8, :] = hv_new
-            q.C[k:k + 8, :] = jnp.where(quad < 2, hp, hv_new)
+            q.hv[k:k + 8, :] = q.hv[k:k + 8, :] - q.hbj[k:k + 8, :] * (
+                own_p[k:k + 8, :] - halo_p[k:k + 8, :]
+            )
 
         def explicit(g, A):
             for r in range(4):
@@ -631,7 +633,7 @@
                 put(q.hu, 8 + row, at(q.hu, 8 + row) - at(q.hbi, 8 + row) * (
                     at(i_low, 8 + row) - at(i_down, 8 + row)
                 ))
-            c = at(q.C, g * 8)
+            c = at(q.hv, g * 8)
             acc = zero
             for j in reversed(range(GROUP)):
                 pp, uu, vv, ww = pair(p, g, j), pair(q.us, g, j), pair(q.vs, g, j), pair(w, g, j)
@@ -648,8 +650,8 @@
                 newA, hs, pss, vn = [], [], [], []
                 for m in range(2):
                     edge = roll(c, 126 - 4 * (2 * j + m), 1)
-                    pj = jnp.where(lane >= 126, edge, roll(pp[m], 126, 1))
-                    v_new = vv[m] - bbj[m] * (pj - pp[m])
+                    v_new = vv[m] - bbj[m] * (roll(pp[m], 126, 1) - pp[m])
+                    v_new = jnp.where(lane >= 126, edge, v_new)
                     vm = jnp.where(lane < 2, edge, roll(v_new, 2, 1))
                     star = pp[m] - (CH * ss[m]) * ((un[m] - um[m]) + (v_new - vm))
                     dw = dd[m] * ww[m]

time: 30.9 us -> 30.1 us (0.974)
  Pallas kernels: 30.1 us -> 29.3 us
    pallas_call x1, Pallas kernels: 28.7 us -> 28 us  [shards(): pl.pallas_call(functools.partial(kernel, tuple(held), K, nx, ny, nz), out...]
where the time goes in v3:
time: 30.1 us; the launch traced here: 30 us
  Pallas kernels  29.3 us (97%)
  between operations  0.64 us (2%)
    pallas_call x1, Pallas kernels, shards(): pl.pallas_call(functools.partial(kernel, tuple(held), K, nx, ny, nz), out...  28 us
    pallas_call x1, Pallas kernels, shards(): pl.pallas_call(store, out_shape=[jax.ShapeDtypeStruct((R, J), F32)] * 4,...  1.35 us

profile of v3, /device:TPU:0, one launch (start us, length us, event | category | flops | bytes accessed | tf_op | source)
XLA Modules:
  0.0 30.0 jit_solution(2745414344750739642)
XLA Ops:
  0.6 28.0 %shard_map.93 = (f32[1024,128]{1,0:T(8,128)S(1)}, f32[1024,128]{1,0:T(8,128)S(1)}, f32[1024,128]{1,0:T(8,128)S(1)}, f32[1024,128]{1,0:T(8,128)S(1)}) custom-call(f32[1024,128]{1,0:T(8,128)} %bitcast.10, f32[1024,128]{1,0:T(8,128)} %bitcast.11, f32[1024,128]{1,0:T(8,128)} %bitcast.12, f32[1024,128]{1,0:T(8,128)} %bitcast.13, f32[1024,128]{1,0:T(8,128)} %bitcast.14, ...), custom_call_target="tpu_custom_call" | custom-call | tf_op jit(solution)/shard_map/pallas_call | solution.py:816
  28.6 1.3 %shard_map.94 = (f32[1024,128]{1,0:T(8,128)}, f32[1024,128]{1,0:T(8,128)}, f32[1024,128]{1,0:T(8,128)}, f32[1024,128]{1,0:T(8,128)}) custom-call(f32[1024,128]{1,0:T(8,128)S(1)} %get-tuple-element.12.u, f32[1024,128]{1,0:T(8,128)S(1)} %get-tuple-element.13.v, f32[1024,128]{1,0:T(8,128)S(1)} %get-tuple-element.14.w, f32[1024,128]{1,0:T(8,128)S(1)} %get-tuple-element.15.p), custom_call_target="tpu_custom_call" | custom-call | tf_op jit(solution)/shard_map/pallas_call | solution.py:824

commit v4 on v3

--- a/solution.py
+++ b/solution.py
@@ -545,8 +545,8 @@
             low, high, col = lows[n], highs[n], cols[n]
             for r in (4, 2):
                 low, high = low + roll(low, r, 0), high + roll(high, r, 0)
-            for r in (64, 32, 16, 8):
-                col = col + roll(col, r, 1)
+            for r in (32, 8):
+                col = (col + roll(col, r, 1)) + (roll(col, 2 * r, 1) + roll(col, 3 * r, 1))
             rows[0] = rows[0] - jnp.where(sub < 2, CH * low, 0.0)
             rows[1] = rows[1] - jnp.where(sub >= 6, CH * high, 0.0)
             for m in range(2):
@@ -707,14 +707,19 @@
                 level_sums()
             columns_without(q.Ow.at[t], q.Oc, q.Ob.at[t])
             rows_without(q.iw_low.at[t], q.is_low, q.b_low.at[t])
-            for c in works:
-                c.wait()
-            for n in range(2):
-                open_up(q.jw_fl.at[t], q.jw_fr.at[t], n * KH, q.Hw.at[t], n * KJ)
-            columns_without(q.Hw.at[t], q.Hc, q.Hb.at[t])
-            rows_without(q.iw_up.at[t], q.is_up, q.b_up.at[t])
-            rows_without(q.iw_down.at[t], q.is_down, q.b_down.at[t])
-            halo_rows(t, A1, W1)
+
+            def finish(A, W):
+                for c in works:
+                    c.wait()
+                for n in range(2):
+                    open_up(q.jw_fl.at[t], q.jw_fr.at[t], n * KH, q.Hw.at[t], n * KJ)
+                columns_without(q.Hw.at[t], q.Hc, q.Hb.at[t])
+                rows_without(q.iw_up.at[t], q.is_up, q.b_up.at[t])
+                rows_without(q.iw_down.at[t], q.is_down, q.b_down.at[t])
+                halo_rows(t, A, W)
+
+            if t == 0:
+                finish(A1, W1)
 
         if final:
             def emit(g, carry):
@@ -754,7 +759,12 @@
             for n, v in enumerate((wb2, pa2)):
                 a0, a1, b0, b1 = (roll(v[m], k, 0) for k in (6, 2) for m in range(2))
                 above, below = roll(halo_up, 6 - 2 * n, 0), roll(halo_down, -2 * n, 0)
-                edges = [insert(halo_j, 8 * n + 4 * m) for m in range(2)]
+                edges = [
+                    jnp.where(
+                        lane >= 126, roll(fr, 124 - 8 * n - 4 * m, 1), roll(fl, -8 * n - 4 * m, 1)
+                    )
+                    for m in range(2)
+                ]
                 stencil.append((
                     v,
                     (jnp.where(sub < 6, a0, a1), jnp.where(sub < 6, a1, above)),
@@ -776,7 +786,10 @@
                             sum(terms[k + 1:k + 2], terms[k]) for k in range(0, len(terms), 2)
                         ]
                     halves_.append(terms[0])
-                rows.append(jnp.concatenate(halves_, 0))
+                rows.append(halves_)
+            if t:
+                finish(*rows)
+            rows = [jnp.concatenate(r, 0) for r in rows]
             sends, wb_own, pa_own = send_round(t + 1, rows[1], rows[0])
 
         def implicit(g, wprev, wb2=wb2, pa2=pa2):

time: 30.1 us -> 29.7 us (0.987)
  Pallas kernels: 29.3 us -> 28.9 us
    pallas_call x1, Pallas kernels: 28 us -> 27.6 us  [shards(): pl.pallas_call(functools.partial(kernel, tuple(held), K, nx, ny, nz), out...]
where the time goes in v4:
time: 29.7 us; the launch traced here: 29.6 us
  Pallas kernels  28.9 us (97%)
  between operations  0.64 us (2%)
    pallas_call x1, Pallas kernels, shards(): pl.pallas_call(functools.partial(kernel, tuple(held), K, nx, ny, nz), out...  27.6 us
    pallas_call x1, Pallas kernels, shards(): pl.pallas_call(store, out_shape=[jax.ShapeDtypeStruct((R, J), F32)] * 4,...  1.35 us

profile of v4, /device:TPU:0, one launch (start us, length us, event | category | flops | bytes accessed | tf_op | source)
XLA Modules:
  0.0 29.6 jit_solution(15728405680510826493)
XLA Ops:
  0.6 27.6 %shard_map.93 = (f32[1024,128]{1,0:T(8,128)S(1)}, f32[1024,128]{1,0:T(8,128)S(1)}, f32[1024,128]{1,0:T(8,128)S(1)}, f32[1024,128]{1,0:T(8,128)S(1)}) custom-call(f32[1024,128]{1,0:T(8,128)} %bitcast.10, f32[1024,128]{1,0:T(8,128)} %bitcast.11, f32[1024,128]{1,0:T(8,128)} %bitcast.12, f32[1024,128]{1,0:T(8,128)} %bitcast.13, f32[1024,128]{1,0:T(8,128)} %bitcast.14, ...), custom_call_target="tpu_custom_call" | custom-call | tf_op jit(solution)/shard_map/pallas_call | solution.py:829
  28.2 1.3 %shard_map.94 = (f32[1024,128]{1,0:T(8,128)}, f32[1024,128]{1,0:T(8,128)}, f32[1024,128]{1,0:T(8,128)}, f32[1024,128]{1,0:T(8,128)}) custom-call(f32[1024,128]{1,0:T(8,128)S(1)} %get-tuple-element.12.u, f32[1024,128]{1,0:T(8,128)S(1)} %get-tuple-element.13.v, f32[1024,128]{1,0:T(8,128)S(1)} %get-tuple-element.14.w, f32[1024,128]{1,0:T(8,128)S(1)} %get-tuple-element.15.p), custom_call_target="tpu_custom_call" | custom-call | tf_op jit(solution)/shard_map/pallas_call | solution.py:837

commit v5 on v4

--- a/solution.py
+++ b/solution.py
@@ -13,6 +13,7 @@
 GAIN = 4096.0
 MESH = pl.DeviceIdType.MESH
 GROUP = 16
+CHUNKS = 2
 F32 = jnp.float32
 
 
@@ -22,7 +23,7 @@
     D = lambda *s: pltpu.SemaphoreType.DMA(s)
     m = max(nz - 1, 1)
     s = {n: V(R) for n in (
-        "us", "vs", "s", "bi", "bj", "E", "D", "H", "X", "Y", "ps", "h",
+        "us", "vs", "p", "bi", "bj", "E", "D", "H", "h",
         "dX", "dY", "P", "Q", "XG", "YG",
     )}
     s |= {n: V(3 * K2 + 16) for n in ("i0_low", "i0_high", "i0_up", "i0_down")}
@@ -54,8 +55,9 @@
     return s
 
 
-def kernel(names, K, nx, ny, nz, u_in, v_in, w_in, p_in, b_in, s_in, uo, vo, w, p, *refs):
-    q = SimpleNamespace(**dict(zip(names, refs)))
+def kernel(names, K, nx, ny, nz, u_in, v_in, w_in, p_in, b_in, s_in, uo, vo, w, ps, s, X, Y, wend, *refs):
+    q = SimpleNamespace(**dict(zip(names, refs)), ps=ps, s=s, X=X, Y=Y)
+    p = q.p
     gx, gy, me = lax.axis_index("gx"), lax.axis_index("gy"), lax.axis_index("lev")
     up, down = lax.rem(gx + 1, nx), lax.rem(gx + nx - 1, nx)
     right, left = lax.rem(gy + 1, ny), lax.rem(gy + ny - 1, ny)
@@ -803,16 +805,38 @@
                 wprev = wn
             return wprev
 
-    each(implicit, wb2)
-
-
-def store(u, v, w, p, u_out, v_out, w_out, p_out, sem):
-    copies = [
-        pltpu.make_async_copy(src, dst, sem.at[n])
-        for n, (src, dst) in enumerate(((u, u_out), (v, v_out), (w, w_out), (p, p_out)))
-    ]
-    for c in copies:
+    wend[0:16, :], wend[16:32, :] = wb, pa
+
+
+def store(K, u, v, w, ps, s, X, Y, wend, u_out, v_out, w_out, p_out, wf, pf, sem):
+    copies = []
+
+    def begin(src, dst, n):
+        c = pltpu.make_async_copy(src, dst, sem.at[n])
         c.start()
+        copies.append(c)
+
+    begin(u, u_out, 0)
+    begin(v, v_out, 1)
+    wb, pa = ((wend[16 * n:16 * n + 8, :], wend[16 * n + 8:16 * n + 16, :]) for n in range(2))
+    before, size = wb, 16 * K // CHUNKS
+
+    def step(k, before):
+        after = []
+        for m in range(2):
+            rows = pl.ds(pl.multiple_of(k * 16 + 8 * m, 8), 8)
+            wn = w[rows, :] + X[rows, :] * wb[m] + Y[rows, :] * pa[m]
+            wf[rows, :] = wn
+            pf[rows, :] = ps[rows, :] - s[rows, :] * (wn - before[m])
+            after.append(wn)
+        return tuple(after)
+
+    for n in range(CHUNKS):
+        part = K // CHUNKS
+        before = lax.fori_loop(n * part, (n + 1) * part, step, before, unroll=8)
+        rows = pl.ds(n * size, size)
+        begin(wf.at[rows], w_out.at[rows], 2 + 2 * n)
+        begin(pf.at[rows], p_out.at[rows], 3 + 2 * n)
     for c in copies:
         c.wait()
 
@@ -828,18 +852,21 @@
         held = scratch(K, J, nz)
         outs = pl.pallas_call(
             functools.partial(kernel, tuple(held), K, nx, ny, nz),
-            out_shape=[full] * 4,
+            out_shape=[full] * 7 + [pltpu.VMEM((32, J), F32)],
             in_specs=[pl.BlockSpec(memory_space=pl.ANY)] * 6,
-            out_specs=[pl.BlockSpec(memory_space=pltpu.VMEM)] * 4,
+            out_specs=[pl.BlockSpec(memory_space=pltpu.VMEM)] * 8,
             scratch_shapes=list(held.values()),
-            compiler_params=pltpu.CompilerParams(collective_id=0, has_side_effects=True),
+            compiler_params=pltpu.CompilerParams(
+                collective_id=0, has_side_effects=True, vmem_limit_bytes=60 * 2**20
+            ),
         )(*(f.reshape(R, J) for f in fields))
         outs = pl.pallas_call(
-            store,
+            functools.partial(store, K),
             out_shape=[jax.ShapeDtypeStruct((R, J), F32)] * 4,
-            in_specs=[pl.BlockSpec(memory_space=pltpu.VMEM)] * 4,
+            in_specs=[pl.BlockSpec(memory_space=pltpu.VMEM)] * 8,
             out_specs=[pl.BlockSpec(memory_space=pl.ANY)] * 4,
-            scratch_shapes=[pltpu.SemaphoreType.DMA((4,))],
+            scratch_shapes=[full, full, pltpu.SemaphoreType.DMA((2 + 2 * CHUNKS,))],
+            compiler_params=pltpu.CompilerParams(vmem_limit_bytes=16 * 2**20),
         )(*(pltpu.with_memory_space_constraint(o, pltpu.VMEM) for o in outs))
         return tuple(o.reshape(K, I, J) for o in outs)
 

time: 29.7 us -> 29.6 us (level)
  no operation moved by 1% of the time
where the time goes in v5:
time: 29.6 us; the launch traced here: 29.5 us
  Pallas kernels  28.8 us (97%)
  between operations  0.64 us (2%)
    pallas_call x1, Pallas kernels, shards(): pl.pallas_call(functools.partial(kernel, tuple(held), K, nx, ny, nz), out...  27.5 us
    pallas_call x1, Pallas kernels, shards(): pl.pallas_call(functools.partial(store, K), out_shape=[jax.ShapeDtypeStru...  1.36 us

profile of v5, /device:TPU:0, one launch (start us, length us, event | category | flops | bytes accessed | tf_op | source)
XLA Modules:
  0.0 29.5 jit_solution(8351332403529244270)
XLA Ops:
  0.6 27.5 %shard_map.93 = (f32[1024,128]{1,0:T(8,128)S(1)}, f32[1024,128]{1,0:T(8,128)S(1)}, f32[1024,128]{1,0:T(8,128)S(1)}, f32[1024,128]{1,0:T(8,128)S(1)}, f32[1024,12...) custom-call(f32[1024,128]{1,0:T(8,128)} %bitcast.10, ...), custom_call_target="tpu_custom_call" | custom-call | tf_op jit(solution)/shard_map/pallas_call | solution.py:853
  28.1 1.4 %shard_map.94 = (f32[1024,128]{1,0:T(8,128)}, f32[1024,128]{1,0:T(8,128)}, f32[1024,128]{1,0:T(8,128)}, f32[1024,128]{1,0:T(8,128)}) custom-call(f32[1024,128]{1,0:T(8,128)S(1)} %get-tuple-element.16.u, f32[1024,128]{1,0:T(8,128)S(1)} %get-tuple-element.17.v, f32[1024,128]{1,0:T(8,128)S(1)} %get-tuple-element.18.w, f32[1024,128]{1,0:T(8,128)S(1)} %get-tuple-element.19.ps, ...), custom_call_target="tpu_custom_call" | custom-call | tf_op jit(solution)/shard_map/pallas_call | solution.py:863
